TPU v7x, 256 devices: a whole 4x4x8 slice. The times are simulated.
256 devices in a mesh: gx: 16 (over z, y_lo), gy: 4 (over x), gz: 4 (over y_hi, core).
Axes of the slice: x: 4, y: 4 (y_hi: 2, y_lo: 2; y = y_hi * 2 + y_lo), z: 8, core: 2. Of those that a mesh axis runs over, the one named last changes fastest.
Arguments:
- pair_map: bfloat16 [1280, 1280, 128], P('gx', ('gy', 'gz')), may hold values from -6 to 6
- residue_mask: int32 [1280], replicated, may hold values 0 or 1
- proj_weight: bfloat16 [128, 512], replicated, may hold values from -0.5 to 0.5
- gate_weight: bfloat16 [128, 128], replicated, may hold values from -0.5 to 0.5
- out_weight: bfloat16 [128, 128], replicated, may hold values from -0.5 to 0.5
Outputs:
- update: bfloat16 [1280, 1280, 128], P('gx', ('gy', 'gz'))
All inputs are finite; a program needn't handle non-finite values.
Results may differ from a plain program's by a relative error of at most 0.009.
Values may be sent and summed in bfloat16 or wider, within the bound.
A program may use at most 128 MiB of HBM per device.

v0:
```python
import jax
import jax.numpy as jnp
from jax import lax
from jax.sharding import PartitionSpec as P

epsilon = 1.0


def partner_2(x, axis, bit):
    return lax.ppermute(x, axis, [(i, i ^ 1 << bit) for i in range(lax.axis_size(axis))])


def layer_norm_lead(values):
    average = jnp.mean(values, axis=0, keepdims=True)
    centred = values - average
    variance = jnp.mean(centred * centred, axis=0, keepdims=True)
    return centred * lax.rsqrt(variance + epsilon)


def layer_norm_last(values):
    average = jnp.mean(values, axis=-1, keepdims=True)
    centred = values - average
    variance = jnp.mean(centred * centred, axis=-1, keepdims=True)
    return centred * lax.rsqrt(variance + epsilon)


def swap_with(values, bit):
    return partner_2(values, "gx", bit)


def pair_join(values, bit, position):
    partner = swap_with(values, bit)
    mine_first = position // 2**bit % 2 == 0
    return jnp.where(
        mine_first,
        jnp.concatenate([values, partner], axis=1),
        jnp.concatenate([partner, values], axis=1),
    )


def whole_channels(gathered, out_weight, gate_value):
    hidden, row_count, col_count = gathered.shape
    normed_tri = layer_norm_lead(gathered.astype(jnp.float32)).astype(jnp.bfloat16)
    mixed_out = lax.dot_general(
        normed_tri.reshape(hidden, row_count * col_count),
        out_weight,
        (((0,), (0,)), ((), ())),
        preferred_element_type=jnp.float32,
    )
    return gate_value * mixed_out.reshape(row_count, col_count, out_weight.shape[1])


def local(pair_map, residue_mask, proj_weight, gate_weight, out_weight):
    row_count, col_count, chan_count = pair_map.shape
    hidden = out_weight.shape[0]
    residues = residue_mask.shape[0]
    along_x = lax.axis_size("gx")
    along_y = lax.axis_size("gy")
    along_z = lax.axis_size("gz")
    mask_float = residue_mask.astype(jnp.float32)
    row_mask = lax.dynamic_slice_in_dim(mask_float, lax.axis_index("gx") * row_count, row_count)
    col_mask = lax.dynamic_slice_in_dim(
        mask_float, (lax.axis_index("gy") * along_z + lax.axis_index("gz")) * col_count, col_count
    )
    normed = layer_norm_last(pair_map.astype(jnp.float32)).astype(jnp.bfloat16)
    flattened = normed.reshape(row_count * col_count, chan_count)
    projected = lax.dot_general(
        proj_weight, flattened, (((0,), (1,)), ((), ())), preferred_element_type=jnp.float32
    ).reshape(4 * hidden, row_count, col_count)
    pair_mask = (row_mask[:, None] * col_mask[None, :])[None, :, :]
    left_proj = (
        jax.nn.sigmoid(projected[:hidden]) * projected[hidden : 2 * hidden] * pair_mask
    ).astype(jnp.bfloat16)
    right_proj = (
        jax.nn.sigmoid(projected[2 * hidden : 3 * hidden]) * projected[3 * hidden :] * pair_mask
    ).astype(jnp.bfloat16)
    gate_value = jax.nn.sigmoid(
        jnp.dot(flattened, gate_weight, preferred_element_type=jnp.float32)
    ).reshape(row_count, col_count, chan_count)
    group_count = along_y * along_z
    group_chan = hidden // group_count
    left_group, right_group = (
        lax.all_to_all(left_proj, ("gy", "gz"), split_axis=0, concat_axis=2, tiled=True),
        lax.all_to_all(right_proj, ("gy", "gz"), split_axis=0, concat_axis=2, tiled=True),
    )
    levels = along_x.bit_length() - 1
    low_bits = levels // 2
    high_count = 2 ** (levels - low_bits)
    low_count = 2**low_bits
    position = lax.axis_index("gx")
    left_tile = left_group
    for bit in range(low_bits):
        left_tile = pair_join(left_tile, bit, position)
    right_tile = right_group
    for bit in range(low_bits, levels):
        right_tile = pair_join(right_tile, bit, position)
    block_tile = jnp.einsum(
        "cik,cjk->cij", left_tile, right_tile, preferred_element_type=jnp.float32
    ).astype(jnp.bfloat16)
    for bit in range(low_bits):
        current = block_tile.shape[1]
        span = block_tile.shape[2]
        shaped = block_tile.reshape(group_chan, current // (2 * row_count), 2, row_count, span)
        own_bit = position // 2**bit % 2
        kept = lax.dynamic_index_in_dim(shaped, own_bit, axis=2, keepdims=False).reshape(
            group_chan, current // 2, span
        )
        sent = lax.dynamic_index_in_dim(shaped, 1 - own_bit, axis=2, keepdims=False).reshape(
            group_chan, current // 2, span
        )
        arrived = swap_with(sent, bit)
        block_tile = jnp.where(
            own_bit == 0,
            jnp.concatenate([kept, arrived], axis=2),
            jnp.concatenate([arrived, kept], axis=2),
        )
    block_tile = (
        block_tile.reshape(group_chan, row_count, low_count, high_count, row_count)
        .transpose(0, 1, 3, 2, 4)
        .reshape(group_chan, row_count, residues)
    )
    gathered = lax.all_to_all(block_tile, ("gy", "gz"), split_axis=2, concat_axis=0, tiled=True)
    update = whole_channels(gathered, out_weight, gate_value)
    return update.astype(jnp.bfloat16)


def solution(mesh):
    placed = (P("gx", ("gy", "gz"), None), P(), P(), P(), P())
    return jax.shard_map(
        local, mesh=mesh, in_specs=placed, out_specs=P("gx", ("gy", "gz"), None), check_vma=False
    )
```

profile of v0, /device:TPU:1, one launch (start us, length us, event | category | flops | bytes accessed | tf_op | source)
XLA Modules:
  0.0 544.5 jit_solution(5831082442729359485)
XLA Ops:
  0.0 0.0 copy-start
  0.0 0.8 convert_element_type.46
  0.8 2.2 convert_reduce_fusion
  3.1 3.5 fusion.18
  6.6 0.0 copy-done.3
  6.6 2.1 fusion.19
  8.7 0.0 copy-start.4
  8.7 1.2 copy-done.4
  9.9 0.0 copy-done
  9.9 1.8 convolution_bitcast_fusion
  11.7 3.0 slice_multiply_fusion.1
  14.7 5.5 %copy.36 = f32[128,80,80]{2,1,0:T(8,128)} copy(f32[128,80,80]{0,2,1:T(8,128)} %bitcast.48) | data formatting | bytes 6553600 | tf_op jit(solution)/shard_map/mul | solution.py:72
  20.2 4.5 copy.38
  24.6 0.1 fusion.31
  24.7 0.1 broadcast_multiply_fusion
  24.8 6.4 %multiply_convert_fusion.1 = (bf16[128,80,80]{2,1,0:T(8,128)(2,1)S(1)}, bf16[128,80,80]{2,1,0:T(8,128)(2,1)}) fusion(f32[128,80,80]{2,1,0:T(8,128)} %copy.36, f32[80,80]{1,0:T(8,128)S(1)} %broadcast_multiply_fusion, f32[128,80,80]{2,1,0:T(8,128)} %copy.38), kind=kLoop, calls=%fused_computation.22 | loop fusion | flops 3276800 | bytes 9856000 | tf_op jit(solution)/shard_map/convert_element_type | solution.py:73
  31.2 42.0 %all_to_all.45 = bf16[128,80,80]{2,1,0:T(8,128)(2,1)} all-to-all(bf16[128,80,80]{2,1,0:T(8,128)(2,1)S(1)} %get-tuple-element.11), channel_id=1, replica_groups=mesh['gx'=16,'gy'=4,'gz'=4] {'gy','gz'}, dimensions={0} | all-to-all | bytes 3276800 | tf_op jit(solution)/shard_map/all_to_all | solution.py:83
  73.2 4.7 all-to-all-start.1
  78.0 4.9 copy.37
  82.9 5.2 all_to_all.36
  88.1 0.4 collective-permute-start
  88.5 23.5 %all-to-all-done.1 = bf16[128,80,80]{2,1,0:T(8,128)(2,1)S(1)} async-done(((bf16[128,80,80]{2,1,0:T(8,128)(2,1)}), bf16[128,80,80]{2,1,0:T(8,128)(2,1)S(1)}, u32[]{:S(2)}, u32[]{:S(2)}) %all-to-all-start.1) | async-done | bytes 1638432 | tf_op jit(solution)/shard_map/all_to_all | solution.py:84
  112.0 3.2 copy.39
  115.2 4.4 all_to_all.40
  119.6 3.1 collective-permute-start.2
  122.7 20.7 %collective-permute-done = bf16[8,80,1280]{2,1,0:T(8,128)(2,1)} collective-permute-done((bf16[8,80,1280]{2,1,0:T(8,128)(2,1)}, bf16[8,80,1280]{2,1,0:T(8,128)(2,1)}, u32[]{:S(2)}, u32[]{:S(2)}) %collective-permute-start) | collective-permute-done | bytes 1638432 | tf_op jit(solution)/shard_map/ppermute | solution.py:10
  143.4 0.0 copy-done.5
  143.4 3.8 maximum_select_fusion.4
  147.2 1.6 collective-permute-start.1
  148.8 44.3 %collective-permute-done.2 = bf16[8,80,1280]{2,1,0:T(8,128)(2,1)} collective-permute-done((bf16[8,80,1280]{2,1,0:T(8,128)(2,1)S(1)}, bf16[8,80,1280]{2,1,0:T(8,128)(2,1)}, u32[]{:S(2)}, u32[]{:S(2)}) %collective-permute-start.2) | collective-permute-done | bytes 1638432 | tf_op jit(solution)/shard_map/ppermute | solution.py:10
  193.1 3.9 maximum_select_fusion.5
  197.0 6.9 %collective-permute-start.3 = (bf16[8,160,1280]{2,1,0:T(8,128)(2,1)}, bf16[8,160,1280]{2,1,0:T(8,128)(2,1)}, u32[]{:S(2)}, u32[]{:S(2)}) collective-permute-start(bf16[8,160,1280]{2,1,0:T(8,128)(2,1)} %maximum_select_fusion.5), channel_id=1, source_target_pairs={{0,128},{16,144},{32,160},{48,176},{64,192},{80,208},{96,224},{112... | collective-permute-start | bytes 9830408 | tf_op jit(solution)/shard_map/ppermute | solution.py:10
  203.9 119.5 %collective-permute-done.1 = bf16[8,160,1280]{2,1,0:T(8,128)(2,1)} collective-permute-done((bf16[8,160,1280]{2,1,0:T(8,128)(2,1)}, bf16[8,160,1280]{2,1,0:T(8,128)(2,1)}, u32[]{:S(2)}, u32[]{:S(2)}) %collective-permute-start.1) | collective-permute-done | bytes 3276832 | tf_op jit(solution)/shard_map/ppermute | solution.py:10
  323.5 0.0 collective-permute-done.3
  323.5 13.0 %fusion.27 = bf16[8,320,320]{2,1,0:T(8,128)(2,1)S(1)} fusion(bf16[8,160,1280]{2,1,0:T(8,128)(2,1)} %collective-permute-done.3, bf16[8,160,1280]{2,1,0:T(8,128)(2,1)} %maximum_select_fusion.5, pred[]{:T(512)S(6)} %eq.23, bf16[8,160,1280]{2,1,0:T(8,128)(2,1)} %collective-permute-done.1, bf16[8,160,1280]{2,1,0:T(8,128)(2,1)} %maximum_select_fusion.4, pred[]{:T(512)S(6)} %eq.21), kind=kOutput, calls=%fused_computation.45 | convolution fusion | flops 2156953600 | bytes 14745602 | tf_op jit(solution)/shard_map/cik,cjk->cij/dot_general | solution.py:97
  336.5 1.2 dynamic-slice_bitcast_fusion
  337.6 0.0 collective-permute-start.4
  337.6 21.1 %collective-permute-done.4 = bf16[8,160,320]{2,1,0:T(8,128)(2,1)S(1)} collective-permute-done((bf16[8,160,320]{2,1,0:T(8,128)(2,1)}, bf16[8,160,320]{2,1,0:T(8,128)(2,1)S(1)}, u32[]{:S(2)}, u32[]{:S(2)}) %collective-permute-start.4) | collective-permute-done | bytes 819232 | tf_op jit(solution)/shard_map/ppermute | solution.py:10
  358.7 1.2 maximum_select_fusion.11
  359.9 0.2 constant_dynamic-slice_fusion
  360.1 78.8 %collective-permute-start.5 = (bf16[8,80,640]{2,1,0:T(8,128)(2,1)S(1)}, bf16[8,80,640]{2,1,0:T(8,128)(2,1)S(1)}, u32[]{:S(2)}, u32[]{:S(2)}) collective-permute-start(bf16[8,80,640]{2,1,0:T(8,128)(2,1)S(1)} %get-tuple-element.10), channel_id=1, source_target_pairs={{0,32},{16,48},{32,0},{48,16},{64,96},{80,112},{96,64},{112,80},{1... | collective-permute-start | bytes 2457608 | tf_op jit(solution)/shard_map/ppermute | solution.py:10
  438.9 2.2 concatenate.72
  441.1 14.0 %collective-permute-done.5 = bf16[8,80,640]{2,1,0:T(8,128)(2,1)S(1)} collective-permute-done((bf16[8,80,640]{2,1,0:T(8,128)(2,1)S(1)}, bf16[8,80,640]{2,1,0:T(8,128)(2,1)S(1)}, u32[]{:S(2)}, u32[]{:S(2)}) %collective-permute-start.5) | collective-permute-done | bytes 819232 | tf_op jit(solution)/shard_map/ppermute | solution.py:10
  455.1 2.2 concatenate.73
  457.3 5.6 %fusion.26 = bf16[8,80,4,4,80]{4,2,3,1,0:T(4,128)(2,1)S(1)} fusion(bf16[8,80,2,4,80]{4,3,2,1,0:T(4,128)(2,1)} %concatenate.73, bf16[8,80,2,4,80]{4,3,2,1,0:T(4,128)(2,1)} %concatenate.72, pred[]{:T(512)S(6)} %eq.21), kind=kLoop, calls=%fused_computation.44 | loop fusion | flops 2457600 | bytes 3276801 | tf_op jit(solution)/shard_map/transpose | solution.py:119
  462.9 3.7 copy.45
  466.6 10.6 %all-to-all-start.2 = ((bf16[8,80,1280]{1,0,2:T(8,128)(2,1)}), bf16[8,80,1280]{1,0,2:T(8,128)(2,1)S(1)}, u32[]{:S(2)}, u32[]{:S(2)}) async-start(bf16[8,80,1280]{1,0,2:T(8,128)(2,1)} %bitcast.51), calls=%async_computation.2 | async-start | bytes 5242880 | tf_op jit(solution)/shard_map/all_to_all | solution.py:122
  477.2 0.0 copy-done.7
  477.2 4.3 fusion.2
  481.5 29.7 %all-to-all-done.2 = bf16[8,80,1280]{1,0,2:T(8,128)(2,1)S(1)} async-done(((bf16[8,80,1280]{1,0,2:T(8,128)(2,1)}), bf16[8,80,1280]{1,0,2:T(8,128)(2,1)S(1)}, u32[]{:S(2)}, u32[]{:S(2)}) %all-to-all-start.2) | async-done | bytes 1638432 | tf_op jit(solution)/shard_map/all_to_all | solution.py:122
  511.1 3.2 copy.42
  514.3 6.1 %reshape.190 = f32[8,80,16,80]{3,2,1,0:T(8,128)} reshape(bf16[8,80,1280]{2,1,0:T(8,128)(2,1)} %copy.42) | data formatting | bytes 4915200 | tf_op jit(solution)/shard_map/convert_element_type | solution.py:43
  520.4 3.1 bitcast_reduce_fusion
  523.5 0.9 copy-done.2
  524.4 0.8 multiply_reduce_fusion
  525.2 0.1 div.71
  525.3 0.1 rsqrt.21
  525.4 6.5 %copy.43 = f32[16,8,80,80]{3,2,1,0:T(8,128)} copy(f32[16,8,80,80]{3,0,2,1:T(8,128)} %bitcast.46) | data formatting | bytes 6553600 | tf_op jit(solution)/shard_map/convert_element_type | solution.py:43
  531.9 4.5 reshape.188
  536.4 0.0 copy-start.6
  536.4 1.5 fusion.28
  537.9 2.9 copy.44
  540.8 0.0 copy-start.1
  540.8 3.7 multiply_convert_fusion.2
  (10 shorter events, 0.1 us)
Async XLA Ops:
  0.0 9.9 %copy-start = (bf16[128,512]{1,0:T(8,128)(2,1)S(1)}, bf16[128,512]{1,0:T(8,128)(2,1)}, u32[]{:S(2)}) copy-start(bf16[128,512]{1,0:T(8,128)(2,1)} %param.7) | copy-start | bytes 393220
  0.0 6.6 %copy-start.3 = (bf16[80,80,128]{2,1,0:T(8,128)(2,1)S(1)}, bf16[80,80,128]{2,1,0:T(8,128)(2,1)}, u32[]{:S(2)}) copy-start(bf16[80,80,128]{2,1,0:T(8,128)(2,1)} %param.5) | copy-start | bytes 4915204
  8.7 1.2 copy-start.4
  73.2 38.8 %all-to-all-start.1 = ((bf16[128,80,80]{2,1,0:T(8,128)(2,1)}), bf16[128,80,80]{2,1,0:T(8,128)(2,1)S(1)}, u32[]{:S(2)}, u32[]{:S(2)}) async-start(bf16[128,80,80]{2,1,0:T(8,128)(2,1)} %get-tuple-element.12), calls=%async_computation.1 | async-start | bytes 5242880 | tf_op jit(solution)/shard_map/all_to_all | solution.py:84
  88.1 55.3 %collective-permute-start = (bf16[8,80,1280]{2,1,0:T(8,128)(2,1)}, bf16[8,80,1280]{2,1,0:T(8,128)(2,1)}, u32[]{:S(2)}, u32[]{:S(2)}) collective-permute-start(bf16[8,80,1280]{2,1,0:T(8,128)(2,1)} %all_to_all.36), channel_id=1, source_target_pairs={{0,16},{16,0},{32,48},{48,32},{64,80},{80,64},{96,112},{112,96},{1... | collective-permute-start | bytes 4915208 | tf_op jit(solution)/shard_map/ppermute | solution.py:10
  115.2 28.2 %copy-start.5 = (bf16[8,80,1280]{2,1,0:T(8,128)(2,1)S(1)}, bf16[8,80,1280]{2,1,0:T(8,128)(2,1)}, u32[]{:S(2)}) copy-start(bf16[8,80,1280]{2,1,0:T(8,128)(2,1)} %all_to_all.36) | copy-start | bytes 4915204
  119.6 73.5 %collective-permute-start.2 = (bf16[8,80,1280]{2,1,0:T(8,128)(2,1)S(1)}, bf16[8,80,1280]{2,1,0:T(8,128)(2,1)}, u32[]{:S(2)}, u32[]{:S(2)}) collective-permute-start(bf16[8,80,1280]{2,1,0:T(8,128)(2,1)S(1)} %all_to_all.40), channel_id=1, source_target_pairs={{0,64},{16,80},{32,96},{48,112},{64,0},{80,16},{96,32},{112,48},{1... | collective-permute-start | bytes 4915208 | tf_op jit(solution)/shard_map/ppermute | solution.py:10
  147.2 176.3 %collective-permute-start.1 = (bf16[8,160,1280]{2,1,0:T(8,128)(2,1)}, bf16[8,160,1280]{2,1,0:T(8,128)(2,1)}, u32[]{:S(2)}, u32[]{:S(2)}) collective-permute-start(bf16[8,160,1280]{2,1,0:T(8,128)(2,1)} %maximum_select_fusion.4), channel_id=1, source_target_pairs={{0,32},{16,48},{32,0},{48,16},{64,96},{80,112},{96,64},{112,80},{1... | collective-permute-start | bytes 9830408 | tf_op jit(solution)/shard_map/ppermute | solution.py:10
  197.0 126.4 %collective-permute-start.3 = (bf16[8,160,1280]{2,1,0:T(8,128)(2,1)}, bf16[8,160,1280]{2,1,0:T(8,128)(2,1)}, u32[]{:S(2)}, u32[]{:S(2)}) collective-permute-start(bf16[8,160,1280]{2,1,0:T(8,128)(2,1)} %maximum_select_fusion.5), channel_id=1, source_target_pairs={{0,128},{16,144},{32,160},{48,176},{64,192},{80,208},{96,224},{112... | collective-permute-start | bytes 9830408 | tf_op jit(solution)/shard_map/ppermute | solution.py:10
  337.6 21.1 %collective-permute-start.4 = (bf16[8,160,320]{2,1,0:T(8,128)(2,1)}, bf16[8,160,320]{2,1,0:T(8,128)(2,1)S(1)}, u32[]{:S(2)}, u32[]{:S(2)}) collective-permute-start(bf16[8,160,320]{2,1,0:T(8,128)(2,1)} %bitcast.11), channel_id=1, source_target_pairs={{0,16},{16,0},{32,48},{48,32},{64,80},{80,64},{96,112},{112,96},{1... | collective-permute-start | bytes 2457608 | tf_op jit(solution)/shard_map/ppermute | solution.py:10
  360.1 95.0 %collective-permute-start.5 = (bf16[8,80,640]{2,1,0:T(8,128)(2,1)S(1)}, bf16[8,80,640]{2,1,0:T(8,128)(2,1)S(1)}, u32[]{:S(2)}, u32[]{:S(2)}) collective-permute-start(bf16[8,80,640]{2,1,0:T(8,128)(2,1)S(1)} %get-tuple-element.10), channel_id=1, source_target_pairs={{0,32},{16,48},{32,0},{48,16},{64,96},{80,112},{96,64},{112,80},{1... | collective-permute-start | bytes 2457608 | tf_op jit(solution)/shard_map/ppermute | solution.py:10
  466.6 10.6 %copy-start.7 = (bf16[128,128]{1,0:T(8,128)(2,1)S(1)}, bf16[128,128]{1,0:T(8,128)(2,1)}, u32[]{:S(2)}) copy-start(bf16[128,128]{1,0:T(8,128)(2,1)} %param.8) | copy-start | bytes 98308
  466.6 44.5 %all-to-all-start.2 = ((bf16[8,80,1280]{1,0,2:T(8,128)(2,1)}), bf16[8,80,1280]{1,0,2:T(8,128)(2,1)S(1)}, u32[]{:S(2)}, u32[]{:S(2)}) async-start(bf16[8,80,1280]{1,0,2:T(8,128)(2,1)} %bitcast.51), calls=%async_computation.2 | async-start | bytes 5242880 | tf_op jit(solution)/shard_map/all_to_all | solution.py:122
  520.4 4.0 copy-start.2
  536.4 4.4 copy-start.6
  540.8 3.7 copy-start.1
where the time goes:
time: 547 us; the launch traced here: 545 us
  waiting for transfers between devices  273 us (50%)
  starting transfers between devices  106 us (19%)
  local copies, waits for them, and re-layouts  62.6 us (11%)
  blocking collectives  42 us (8%)
  other arithmetic  38.1 us (7%)
  matrix products  22.8 us (4%)
    ppermute x6, waiting for transfers between devices, partner_2(): lax.ppermute(x, axis, [(i, i ^ 1 << bit) for i in range(lax.axis_size(axi...  220 us
    ppermute x6, starting transfers between devices, partner_2(): lax.ppermute(x, axis, [(i, i ^ 1 << bit) for i in range(lax.axis_size(axi...  90.8 us
    all_to_all x1, blocking collectives, local(): lax.all_to_all(left_proj, ('gy', 'gz'), split_axis=0, concat_axis=2, tile...  42 us
    all_to_all x1, waiting for transfers between devices, local(): lax.all_to_all(block_tile, ('gy', 'gz'), split_axis=2, concat_axis=0, til...  29.7 us
    all_to_all x1, waiting for transfers between devices, local(): lax.all_to_all(right_proj, ('gy', 'gz'), split_axis=0, concat_axis=2, til...  23.5 us
    convert_element_type x3, local copies, waits for them, and re-layouts, whole_channels(): gathered.astype(jnp.float32)  17 us
    dot_general x1, matrix products, local(): jnp.einsum('cik,cjk->cij', left_tile, right_tile, preferred_element_type=...  13 us
  transfers between devices with their start and end apart: 8, of which 7 were waited for; matrix products, arithmetic and copies ran while one was open for 4% of the time, Pallas kernels for 0%

commit v1 on v0

v1 whole, which is shorter than its diff:
```python
import jax
import jax.numpy as jnp
from jax import lax
from jax.experimental import pallas as pl
from jax.experimental.pallas import tpu as pltpu
from jax.sharding import PartitionSpec as P

MESH = pl.DeviceIdType.MESH
EPS = 1.0
LANES = 128
BLOCK = 80
SUB = 8
SEGS = BLOCK // SUB
TILES = -(-SEGS * BLOCK // LANES)
WIDE = TILES * LANES
CHIPS = 128
BF16 = jnp.bfloat16
F32 = jnp.float32
ANY = pl.BlockSpec(memory_space=pl.ANY)
VMEM = pl.BlockSpec(memory_space=pltpu.VMEM)
BIG = 60 * 2**20


def place():
    gx, gy, gz = lax.axis_index("gx"), lax.axis_index("gy"), lax.axis_index("gz")
    return gy, (gz // 2) * 2 + gx % 2, gx // 2, gz % 2


def device(x, y, z, core):
    return (z * 2 + y % 2, x, (y // 2) * 2 + core)


def layer_norm(values, axis):
    average = jnp.mean(values, axis=axis, keepdims=True)
    centred = values - average
    variance = jnp.mean(centred * centred, axis=axis, keepdims=True)
    return centred * lax.rsqrt(variance + EPS)


def project_kernel(pair_ref, mask_ref, weight_ref, normed_ref, message_ref, left, right):
    def norm_rows(sub, _):
        for seg in range(SEGS):
            rows = pair_ref[SUB * seg + sub].astype(F32)
            normed_ref[sub, pl.ds(seg * BLOCK, BLOCK), :] = layer_norm(rows, -1).astype(BF16)
        normed_ref[sub, pl.ds(SEGS * BLOCK, WIDE - SEGS * BLOCK), :] = jnp.zeros(
            (WIDE - SEGS * BLOCK, LANES), BF16
        )
        for tile in range(TILES):
            block = normed_ref[sub, pl.ds(tile * LANES, LANES), :]
            projected = lax.dot_general(
                weight_ref[...], block, (((1,), (1,)), ((), ())), preferred_element_type=F32
            )
            mask = mask_ref[sub, :, pl.ds(tile * LANES, LANES)]
            first, second, third, fourth = (projected[128 * n : 128 * n + 128] for n in range(4))
            start = tile * SUB + sub
            left[pl.ds(start, CHIPS, stride=TILES * SUB), :] = jax.nn.sigmoid(first) * second * mask
            right[pl.ds(start, CHIPS, stride=TILES * SUB), :] = jax.nn.sigmoid(third) * fourth * mask
        return 0

    lax.fori_loop(0, SUB, norm_rows, 0)

    def pack(channel, _):
        for which, scratch in enumerate((left, right)):
            for tile in range(TILES):
                start = pl.multiple_of((channel * TILES + tile) * SUB, SUB)
                message_ref[channel, which, tile] = scratch[pl.ds(start, SUB), :].astype(BF16)
        return 0

    lax.fori_loop(0, CHIPS, pack, 0)


def project(pair_map, mask, weight):
    return pl.pallas_call(
        project_kernel,
        name="project",
        out_shape=(
            jax.ShapeDtypeStruct((SUB, WIDE, LANES), BF16),
            jax.ShapeDtypeStruct((CHIPS, 2, TILES, SUB, LANES), BF16),
        ),
        in_specs=[VMEM, VMEM, VMEM],
        out_specs=(VMEM, VMEM),
        scratch_shapes=[pltpu.VMEM((CHIPS * TILES * SUB, LANES), F32)] * 2,
        compiler_params=pltpu.CompilerParams(vmem_limit_bytes=BIG),
    )(pair_map, mask, weight)


def spread_kernel(message, arrived, other, send_sem, recv_sem, home_sem, swap_send, swap_recv):
    x, y, z, core = place()
    half = y % 2
    slot = (z * 4 + x) * 4 + (y // 2) * 2 + core

    def send(step, _):
        dz, dx, dy = step % 8, step // 8 % 4, step // 32
        tx, ty, tz = (x + dx) % 4, (y + dy) % 4, (z + dz) % 8
        pltpu.make_async_remote_copy(
            message.at[(tz * 4 + ty) * 4 + tx],
            arrived.at[slot],
            send_sem,
            recv_sem,
            device_id=device(tx, ty, tz, half),
            device_id_type=MESH,
        ).start()
        return 0

    own = message.at[(z * 4 + y) * 4 + x]

    @pl.when(core == half)
    def _():
        pltpu.make_async_copy(own, arrived.at[slot], recv_sem).start()

    @pl.when(core != half)
    def _():
        pltpu.make_async_remote_copy(
            own,
            arrived.at[slot],
            home_sem,
            recv_sem,
            device_id=device(x, y, z, half),
            device_id_type=MESH,
        ).start()

    lax.fori_loop(1, CHIPS, send, 0)
    most = pl.ds(0, CHIPS - 1)
    pltpu.make_async_copy(message.at[most], message.at[most], send_sem).wait()

    @pl.when(core != half)
    def _():
        pltpu.make_async_copy(own, own, home_sem).wait()

    pltpu.make_async_copy(arrived, arrived, recv_sem).wait()
    swap = pltpu.make_async_remote_copy(
        arrived.at[:, 1],
        other,
        swap_send,
        swap_recv,
        device_id=device(x, y, z, 1 - core),
        device_id_type=MESH,
    )
    swap.start()
    swap.wait()


def spread(message):
    return pl.pallas_call(
        spread_kernel,
        name="spread",
        out_shape=(
            jax.ShapeDtypeStruct(message.shape, BF16),
            jax.ShapeDtypeStruct((CHIPS, TILES, SUB, LANES), BF16),
        ),
        in_specs=[ANY],
        out_specs=(ANY, ANY),
        scratch_shapes=[pltpu.SemaphoreType.DMA] * 5,
        compiler_params=pltpu.CompilerParams(has_side_effects=True),
    )(message)


def lane_index():
    return lax.broadcasted_iota(jnp.int32, (SUB, LANES), 1)


def turn(tile, shift):
    shift %= LANES
    return pltpu.roll(tile, shift, 1) if shift else tile


def unpack_into(tiles, target, row, column):
    lanes = lane_index()
    pieces = []
    for seg in range(SEGS):
        first, offset = divmod(seg * BLOCK, LANES)
        piece = turn(tiles[first], -offset)
        if offset + BLOCK > LANES:
            piece = jnp.where(lanes < LANES - offset, piece, turn(tiles[first + 1], -offset))
        pieces.append(jnp.where(lanes < BLOCK, piece, 0.0))
    for pair in range(SEGS // 2):
        both = jnp.concatenate(pieces[2 * pair : 2 * pair + 2], axis=0).astype(BF16)
        target[pl.ds(pl.multiple_of(row + 16 * pair, 16), 16), column] = both


def triangle_kernel(arrived, other, out_ref, left, right, product):
    core = lax.axis_index("gz") % 2
    columns = 16

    def unpack(step, _):
        z, col = step // columns, step % columns
        lanes = pl.ds(pl.multiple_of(col * LANES, LANES), LANES)
        unpack_into(
            [arrived[step, 0, t].astype(F32) for t in range(TILES)], left, z * BLOCK, lanes
        )
        unpack_into(
            [arrived[step, 1, t].astype(F32) for t in range(TILES)],
            right,
            (2 * z + core) * BLOCK,
            lanes,
        )
        unpack_into(
            [other[step, t].astype(F32) for t in range(TILES)],
            right,
            (2 * z + 1 - core) * BLOCK,
            lanes,
        )
        return 0

    lax.fori_loop(0, CHIPS, unpack, 0)
    chunk = 256

    def multiply(step, _):
        start = pl.multiple_of(step * chunk, chunk)
        product[:, pl.ds(start, chunk)] = lax.dot_general(
            left[...],
            right[pl.ds(start, chunk), :],
            (((1,), (1,)), ((), ())),
            preferred_element_type=F32,
        )
        return 0

    lax.fori_loop(0, 1280 // chunk, multiply, 0)

    def pack(step, _):
        z, group = step // 2, step % 2
        lanes = lane_index()
        for seat in range(8):
            low = seat * BLOCK
            tiles = [None] * TILES
            for seg in range(SEGS):
                row = pl.ds(pl.multiple_of(z * BLOCK + seg * SUB, SUB), SUB)
                source = {}

                def lane_tile(number):
                    if number not in source:
                        start = pl.multiple_of(group * 8 * BLOCK + number * LANES, LANES)
                        source[number] = product[row, pl.ds(start, LANES)]
                    return source[number]

                target = seg * BLOCK
                done = 0
                while done < BLOCK:
                    from_tile, from_lane = divmod(low + done, LANES)
                    to_tile, to_lane = divmod(target + done, LANES)
                    run = min(BLOCK - done, LANES - from_lane, LANES - to_lane)
                    piece = turn(lane_tile(from_tile), to_lane - from_lane)
                    if tiles[to_tile] is None:
                        tiles[to_tile] = piece
                    else:
                        tiles[to_tile] = jnp.where(lanes < to_lane, tiles[to_tile], piece)
                    done += run
            for tile in range(TILES):
                out_ref[z * columns + group * 8 + seat, tile] = tiles[tile].astype(BF16)
        return 0

    lax.fori_loop(0, 16, pack, 0)


def triangle(arrived, other):
    return pl.pallas_call(
        triangle_kernel,
        name="triangle",
        out_shape=jax.ShapeDtypeStruct((CHIPS, TILES, SUB, LANES), BF16),
        in_specs=[VMEM, VMEM],
        out_specs=VMEM,
        scratch_shapes=[
            pltpu.VMEM((640, 2048), BF16),
            pltpu.VMEM((1280, 2048), BF16),
            pltpu.VMEM((640, 1280), F32),
        ],
        compiler_params=pltpu.CompilerParams(vmem_limit_bytes=BIG),
    )(arrived, other)


def collect_kernel(blocks, gathered, send_sem, recv_sem):
    x, y, z, core = place()
    channel = (z * 4 + y) * 4 + x

    def send(step, _):
        dz, dx = step % 8, step // 8 % 4
        rest = step // 32
        tz, tx = (z + dz) % 8, (x + dx) % 4
        ty = 2 * ((y // 2 + rest // 2) % 2) + core
        to_core = (core + rest) % 2
        block = blocks.at[(tz * 4 + tx) * 4 + (ty // 2) * 2 + to_core]
        itself = (tz == z) & (tx == x) & (ty == y) & (to_core == core)

        @pl.when(itself)
        def _():
            pltpu.make_async_copy(block, gathered.at[channel], recv_sem).start()

        @pl.when(jnp.logical_not(itself))
        def _():
            pltpu.make_async_remote_copy(
                block,
                gathered.at[channel],
                send_sem,
                recv_sem,
                device_id=device(tx, ty, tz, to_core),
                device_id_type=MESH,
            ).start()

        return 0

    lax.fori_loop(0, CHIPS, send, 0)
    kept = y % 2 == core

    @pl.when(kept)
    def _():
        most = blocks.at[pl.ds(0, CHIPS - 1)]
        pltpu.make_async_copy(most, most, send_sem).wait()

    @pl.when(jnp.logical_not(kept))
    def _():
        pltpu.make_async_copy(blocks, blocks, send_sem).wait()

    pltpu.make_async_copy(gathered, gathered, recv_sem).wait()


def collect(blocks):
    return pl.pallas_call(
        collect_kernel,
        name="collect",
        out_shape=jax.ShapeDtypeStruct(blocks.shape, BF16),
        in_specs=[ANY],
        out_specs=ANY,
        scratch_shapes=[pltpu.SemaphoreType.DMA] * 2,
        compiler_params=pltpu.CompilerParams(has_side_effects=True),
    )(blocks)


def finish_kernel(gathered, normed_ref, gate_weight, out_weight, out_ref, wide, update):
    def widen(channel, _):
        for tile in range(TILES):
            start = pl.multiple_of((channel * TILES + tile) * SUB, SUB)
            wide[pl.ds(start, SUB), :] = gathered[channel, tile].astype(F32)
        return 0

    lax.fori_loop(0, CHIPS, widen, 0)

    def rows_of(sub, _):
        for tile in range(TILES):
            values = wide[pl.ds(tile * SUB + sub, CHIPS, stride=TILES * SUB), :]
            normed_tri = layer_norm(values, 0).astype(BF16)
            mixed = lax.dot_general(
                normed_tri, out_weight[...], (((0,), (0,)), ((), ())), preferred_element_type=F32
            )
            gate = jax.nn.sigmoid(
                jnp.dot(
                    normed_ref[sub, pl.ds(tile * LANES, LANES), :],
                    gate_weight[...],
                    preferred_element_type=F32,
                )
            )
            update[pl.ds(tile * LANES, LANES), :] = (gate * mixed).astype(BF16)
        for seg in range(SEGS):
            out_ref[SUB * seg + sub] = update[pl.ds(seg * BLOCK, BLOCK), :]
        return 0

    lax.fori_loop(0, SUB, rows_of, 0)


def finish(gathered, normed, gate_weight, out_weight):
    return pl.pallas_call(
        finish_kernel,
        name="finish",
        out_shape=jax.ShapeDtypeStruct((BLOCK, BLOCK, LANES), BF16),
        in_specs=[VMEM] * 4,
        out_specs=VMEM,
        scratch_shapes=[
            pltpu.VMEM((CHIPS * TILES * SUB, LANES), F32),
            pltpu.VMEM((WIDE, LANES), BF16),
        ],
        compiler_params=pltpu.CompilerParams(vmem_limit_bytes=BIG),
    )(gathered, normed, gate_weight, out_weight)


def local(pair_map, residue_mask, proj_weight, gate_weight, out_weight):
    mask_float = residue_mask.astype(F32)
    row_mask = lax.dynamic_slice_in_dim(mask_float, lax.axis_index("gx") * BLOCK, BLOCK)
    col = lax.axis_index("gy") * lax.axis_size("gz") + lax.axis_index("gz")
    col_mask = lax.dynamic_slice_in_dim(mask_float, col * BLOCK, BLOCK)
    mask = row_mask.reshape(SEGS, SUB).T[:, :, None] * col_mask[None, None, :]
    mask = jnp.pad(mask.reshape(SUB, 1, SEGS * BLOCK), ((0, 0), (0, 0), (0, WIDE - SEGS * BLOCK)))
    normed, message = project(pair_map, mask, proj_weight.T)
    arrived, other = spread(message)
    blocks = triangle(arrived, other)
    gathered = collect(blocks)
    return finish(gathered, normed, gate_weight, out_weight)


def solution(mesh):
    placed = (P("gx", ("gy", "gz"), None), P(), P(), P(), P())
    return jax.shard_map(
        local, mesh=mesh, in_specs=placed, out_specs=P("gx", ("gy", "gz"), None), check_vma=False
    )
```

time: 547 us -> 208 us (0.38)
  waiting for transfers between devices: 273 us -> 0 us
  Pallas kernels: 0 us -> 204 us
  starting transfers between devices: 106 us -> 0 us
  local copies, waits for them, and re-layouts: 62.6 us -> 2.82 us
  blocking collectives: 42 us -> 0 us
  other arithmetic: 38.1 us -> 0.72 us
  matrix products: 22.8 us -> 0 us
    ppermute x6 -> x0, waiting for transfers between devices: 220 us -> none  [partner_2(): lax.ppermute(x, axis, [(i, i ^ 1 << bit) for i in range(lax.axis_size(axi...]
    pallas_call x0 -> x5, Pallas kernels: none -> 204 us  [the longest x1 106 us: spread(): pl.pallas_call(spread_kernel, name='spread', out_shape=(jax.ShapeDtypeStr...]
    ppermute x6 -> x0, starting transfers between devices: 90.8 us -> none  [partner_2(): lax.ppermute(x, axis, [(i, i ^ 1 << bit) for i in range(lax.axis_size(axi...]
    all_to_all x2 -> x0, waiting for transfers between devices: 53.2 us -> none  [the longest x1 29.7 us: local(): lax.all_to_all(block_tile, ('gy', 'gz'), split_axis=2, concat_axis=0, til...]
    all_to_all x1 -> x0, blocking collectives: 42 us -> none  [local(): lax.all_to_all(left_proj, ('gy', 'gz'), split_axis=0, concat_axis=2, tile...]
    dot_general x4 -> x0, matrix products: 22.8 us -> none  [the longest x1 13 us: local(): jnp.einsum('cik,cjk->cij', left_tile, right_tile, preferred_element_type=...]
    all_to_all x5 -> x0, local copies, waits for them, and re-layouts: 20.9 us -> none  [the longest x2 10.1 us: local(): lax.all_to_all(left_proj, ('gy', 'gz'), split_axis=0, concat_axis=2, tile...]
    convert_element_type x3 -> x0, local copies, waits for them, and re-layouts: 17 us -> none  [whole_channels(): gathered.astype(jnp.float32)]
  transfers between devices with their start and end apart: 8 -> 0, of which waited for: 7 -> 0; matrix products, arithmetic and copies ran while one was open for 4% -> 0% of each run, Pallas kernels for 0% -> 0%
where the time goes in v1:
time: 208 us; the launch traced here: 207 us
  Pallas kernels  204 us (98%)
  local copies, waits for them, and re-layouts  2.82 us (1%)
    pallas_call x1, Pallas kernels, spread(): pl.pallas_call(spread_kernel, name='spread', out_shape=(jax.ShapeDtypeStr...  106 us
    pallas_call x1, Pallas kernels, collect(): pl.pallas_call(collect_kernel, name='collect', out_shape=jax.ShapeDtypeSt...  55.8 us
    pallas_call x1, Pallas kernels, triangle(): pl.pallas_call(triangle_kernel, name='triangle', out_shape=jax.ShapeDtype...  23.7 us
    pallas_call x1, Pallas kernels, project(): pl.pallas_call(project_kernel, name='project', out_shape=(jax.ShapeDtypeS...  11.3 us
    pallas_call x1, Pallas kernels, finish(): pl.pallas_call(finish_kernel, name='finish', out_shape=jax.ShapeDtypeStru...  7.44 us

profile of v1, /device:TPU:1, one launch (start us, length us, event | category | flops | bytes accessed | tf_op | source)
XLA Modules:
  0.0 207.4 jit_solution(1199261876706247972)
XLA Ops:
  0.0 0.7 convert_element_type.5
  0.7 0.1 fusion
  0.8 0.1 mul.41
  0.9 0.1 reshape.40
  0.9 0.1 copy.11
  1.0 0.1 mul.36
  1.1 0.1 mul.44
  1.3 0.6 pad.4.mask_ref
  1.9 1.7 copy.14
  3.6 11.3 %project.1 = (bf16[8,896,128]{2,1,0:T(8,128)(2,1)}, bf16[128,2,7,8,128]{4,3,2,1,0:T(8,128)(2,1)}) custom-call(bf16[80,80,128]{2,1,0:T(8,128)(2,1)} %pair_ref.1, f32[8,1,896]{2,1,0:T(1,128)} %pad.4.mask_ref, bf16[512,128]{1,0:T(8,128)(2,1)} %bitcast.2), custom_call_target="tpu_custom_call" | custom-call | tf_op jit(solution)/shard_map/project/pallas_call | solution.py:73
  14.9 105.6 %spread.1 = (bf16[128,2,7,8,128]{4,3,2,1,0:T(8,128)(2,1)}, bf16[128,7,8,128]{3,2,1,0:T(8,128)(2,1)}) custom-call(bf16[128,2,7,8,128]{4,3,2,1,0:T(8,128)(2,1)} %get-tuple-element.9.message), custom_call_target="tpu_custom_call" | custom-call | tf_op jit(solution)/shard_map/spread/pallas_call | solution.py:144
  120.5 23.7 %triangle.1.blocks = bf16[128,7,8,128]{3,2,1,0:T(8,128)(2,1)} custom-call(bf16[128,2,7,8,128]{4,3,2,1,0:T(8,128)(2,1)} %get-tuple-element.10.arrived, bf16[128,7,8,128]{3,2,1,0:T(8,128)(2,1)} %get-tuple-element.11.other), custom_call_target="tpu_custom_call" | custom-call | tf_op jit(solution)/shard_map/triangle/pallas_call | solution.py:256
  144.1 55.8 %collect.1.gathered = bf16[128,7,8,128]{3,2,1,0:T(8,128)(2,1)} custom-call(bf16[128,7,8,128]{3,2,1,0:T(8,128)(2,1)} %triangle.1.blocks), custom_call_target="tpu_custom_call" | custom-call | tf_op jit(solution)/shard_map/collect/pallas_call | solution.py:317
  200.0 7.4 %finish.1 = bf16[80,80,128]{2,1,0:T(8,128)(2,1)} custom-call(bf16[128,7,8,128]{3,2,1,0:T(8,128)(2,1)} %collect.1.gathered, bf16[8,896,128]{2,1,0:T(8,128)(2,1)} %get-tuple-element.12.normed_ref, bf16[128,128]{1,0:T(8,128)(2,1)} %gate_weight.1, bf16[128,128]{1,0:T(8,128)(2,1)} %out_weight.1), custom_call_target="tpu_custom_call" | custom-call | tf_op jit(solution)/shard_map/finish/pallas_call | solution.py:360
  (2 shorter events, 0.0 us)

commit v2 on v0

v2 whole, which is shorter than its diff:
```python
import jax
import jax.numpy as jnp
from jax import lax
from jax.experimental import pallas as pl
from jax.experimental.pallas import tpu as pltpu
from jax.sharding import PartitionSpec as P

MESH = pl.DeviceIdType.MESH
EPS = 1.0
LANES = 128
BLOCK = 80
SUB = 8
SEGS = BLOCK // SUB
TILES = -(-SEGS * BLOCK // LANES)
WIDE = TILES * LANES
FLAT = SEGS * BLOCK
BOTH = -(-2 * FLAT // LANES)
EDGE, SPLIT = divmod(FLAT, LANES)
CHIPS = 128
QUARTER = 32
HALF = 640
BF16 = jnp.bfloat16
F32 = jnp.float32
ANY = pl.BlockSpec(memory_space=pl.ANY)
VMEM = pl.BlockSpec(memory_space=pltpu.VMEM)
BIG = 60 * 2**20


def place():
    gx, gy, gz = lax.axis_index("gx"), lax.axis_index("gy"), lax.axis_index("gz")
    return gy, (gz // 2) * 2 + gx % 2, gx // 2, gz % 2


def device(x, y, z, core):
    return (z * 2 + y % 2, x, (y // 2) * 2 + core)


def layer_norm(values, axis):
    average = jnp.mean(values, axis=axis, keepdims=True)
    centred = values - average
    variance = jnp.mean(centred * centred, axis=axis, keepdims=True)
    return centred * lax.rsqrt(variance + EPS)


def lane_index():
    return lax.broadcasted_iota(jnp.int32, (SUB, LANES), 1)


def turn(tile, shift):
    shift %= LANES
    return pltpu.roll(tile, shift, 1) if shift else tile


def unpack_into(tiles, start, target, row, column):
    lanes = lane_index()
    pieces = []
    for seg in range(SEGS):
        first, offset = divmod(start + seg * BLOCK, LANES)
        piece = turn(tiles(first), -offset)
        if offset + BLOCK > LANES:
            piece = jnp.where(lanes < LANES - offset, piece, turn(tiles(first + 1), -offset))
        pieces.append(jnp.where(lanes < BLOCK, piece, 0.0))
    for pair in range(SEGS // 2):
        both = jnp.concatenate(pieces[2 * pair : 2 * pair + 2], axis=0).astype(BF16)
        target[pl.ds(pl.multiple_of(row + 16 * pair, 16), 16), column] = both


def exchange_kernel(
    pair_ref,
    mask_ref,
    weight_ref,
    normed_ref,
    gathered,
    wide,
    message,
    arrived,
    left,
    right,
    other,
    total,
    blocks,
    send_sem,
    home_sem,
    recv_sem,
    swap_send,
    swap_recv,
    back_send,
    back_recv,
):
    x, y, z, core = place()
    half = y % 2
    gx, gy, gz = lax.axis_index("gx"), lax.axis_index("gy"), lax.axis_index("gz")
    barrier = pltpu.get_barrier_semaphore()

    def greet(step, _):
        there = ((gx + step // 16) % 16, (gy + step // 4) % 4, (gz + step) % 4)
        pl.semaphore_signal(barrier, inc=1, device_id=there, device_id_type=MESH)
        return 0

    lax.fori_loop(1, 2 * CHIPS, greet, 0)

    def norm_rows(sub, _):
        for seg in range(SEGS):
            rows = pair_ref[SUB * seg + sub].astype(F32)
            normed_ref[sub, pl.ds(seg * BLOCK, BLOCK), :] = layer_norm(rows, -1).astype(BF16)
        normed_ref[sub, pl.ds(FLAT, WIDE - FLAT), :] = jnp.zeros((WIDE - FLAT, LANES), BF16)
        return 0

    lax.fori_loop(0, SUB, norm_rows, 0)

    def quarter(turn_y, _):
        to_y = (y // 2 + turn_y // 2) % 2 * 2 + (y + turn_y) % 2

        def project(sub, _):
            for tile in range(BOTH):
                if tile < EDGE:
                    block = normed_ref[sub, pl.ds(tile * LANES, LANES), :]
                elif tile == EDGE:
                    block = jnp.concatenate(
                        [
                            normed_ref[sub, pl.ds(EDGE * LANES, SPLIT), :],
                            normed_ref[sub, pl.ds(0, LANES - SPLIT), :],
                        ],
                        axis=0,
                    )
                else:
                    start = (tile - EDGE) * LANES - SPLIT
                    block = normed_ref[sub, pl.ds(start, LANES), :]
                value = None
                for side in range(2):
                    if (side == 0 and tile > EDGE) or (side == 1 and tile < EDGE):
                        continue
                    projected = lax.dot_general(
                        weight_ref[to_y, side],
                        block,
                        (((1,), (1,)), ((), ())),
                        preferred_element_type=F32,
                    )
                    gated = jax.nn.sigmoid(projected[:QUARTER]) * projected[QUARTER:]
                    if value is None:
                        value = gated
                    else:
                        lanes = lax.broadcasted_iota(jnp.int32, (QUARTER, LANES), 1)
                        value = jnp.where(lanes < SPLIT, value, gated)
                mask = mask_ref[sub, :, pl.ds(tile * LANES, LANES)]
                wide[pl.ds(tile * SUB + sub, QUARTER, stride=BOTH * SUB), :] = value * mask
            return 0

        lax.fori_loop(0, SUB, project, 0)

        def pack(number, _):
            for tile in range(BOTH):
                start = pl.multiple_of((number * BOTH + tile) * SUB, SUB)
                message[to_y * QUARTER + number, tile] = wide[pl.ds(start, SUB), :].astype(BF16)
            return 0

        lax.fori_loop(0, QUARTER, pack, 0)

        @pl.when(turn_y == 0)
        def _():
            pl.semaphore_wait(barrier, 2 * CHIPS - 1)
            own = message.at[y * QUARTER + z * 4 + x]
            slot = (x * 4 + (y // 2) * 2 + core) * 8 + z

            @pl.when(core == half)
            def _():
                pltpu.make_async_copy(own, arrived.at[slot], recv_sem.at[0]).start()

            @pl.when(core != half)
            def _():
                pltpu.make_async_remote_copy(
                    own,
                    arrived.at[slot],
                    home_sem,
                    recv_sem.at[0],
                    device_id=device(x, y, z, half),
                    device_id_type=MESH,
                ).start()

        def send(step, _):
            dz, dx = step % 8, step // 8
            tx, tz = (x + dx) % 4, (z + dz) % 8
            pltpu.make_async_remote_copy(
                message.at[to_y * QUARTER + tz * 4 + tx],
                arrived.at[(x * 4 + (y // 2) * 2 + core) * 8 + z],
                send_sem,
                recv_sem.at[turn_y // 2 * 4 + dx],
                device_id=device(tx, to_y, tz, half),
                device_id_type=MESH,
            ).start()
            return 0

        lax.fori_loop(jnp.where(turn_y == 0, 1, 0), QUARTER, send, 0)
        return 0

    lax.fori_loop(0, 4, quarter, 0)

    def clear(step, _):
        total[pl.ds(pl.multiple_of(step * 16, 16), 16), :] = jnp.zeros((16, total.shape[1]), F32)
        return 0

    lax.fori_loop(0, 40, clear, 0)

    def swap_of(group):
        return pltpu.make_async_remote_copy(
            right.at[group],
            other.at[group],
            swap_send.at[group],
            swap_recv.at[group],
            device_id=device(x, y, z, 1 - core),
            device_id_type=MESH,
        )

    def multiply(factor, start):
        total[:, pl.ds(start, HALF)] += lax.dot_general(
            left[...],
            factor[...],
            (((1,), (1,)), ((), ())),
            preferred_element_type=F32,
        )

    def take(group, _):
        base = ((x - group) % 4 * 4 + (y // 2 + group // 4) % 2 * 2) * 8
        some = arrived.at[pl.ds(0, 16)]
        pltpu.make_async_copy(some, some, recv_sem.at[group]).wait()

        def unpack(step, _):
            lanes = pl.ds(pl.multiple_of(step // 8 * LANES, LANES), LANES)
            row = step % 8
            seat = (row // 2 - x) % 4 * 2 + (row - y // 2) % 2

            def tile_of(number):
                return arrived[base + step, number].astype(F32)

            unpack_into(tile_of, FLAT, right.at[group], seat * BLOCK, lanes)
            unpack_into(tile_of, 0, left, row * BLOCK, lanes)
            return 0

        lax.fori_loop(0, 16, unpack, 0)
        swap_of(group).start()
        multiply(right.at[group], 0)
        swap_of(group).wait_recv()
        multiply(other.at[group], HALF)
        return 0

    lax.fori_loop(0, 8, take, 0)

    channel = y * QUARTER + z * 4 + x

    def give(side, _):
        to_core = (core + side) % 2
        for seat in range(8):
            dx, dy = seat // 2, seat % 2
            tx, ty = (x + dx) % 4, 2 * ((y // 2 + dy) % 2) + core

            def one(dz, _, seat=seat, tx=tx, ty=ty):
                tz = (z + dz) % 8
                lanes = lane_index()
                tiles = [None] * TILES
                for seg in range(SEGS):
                    row = pl.ds(pl.multiple_of(tz * BLOCK + seg * SUB, SUB), SUB)
                    low, high, done = seat * BLOCK, seg * BLOCK, 0
                    while done < BLOCK:
                        from_tile, from_lane = divmod(low + done, LANES)
                        to_tile, to_lane = divmod(high + done, LANES)
                        start = pl.multiple_of(side * HALF + from_tile * LANES, LANES)
                        piece = turn(total[row, pl.ds(start, LANES)], to_lane - from_lane)
                        if tiles[to_tile] is None:
                            tiles[to_tile] = piece
                        else:
                            tiles[to_tile] = jnp.where(lanes < to_lane, tiles[to_tile], piece)
                        done += min(BLOCK - done, LANES - from_lane, LANES - to_lane)
                block = blocks.at[(side * 8 + seat) * 8 + dz]
                for tile in range(TILES):
                    block[tile] = tiles[tile].astype(BF16)
                itself = (tz == z) & (tx == x) & (ty == y) & (to_core == core)

                @pl.when(itself)
                def _():
                    pltpu.make_async_copy(block, gathered.at[channel], back_recv).start()

                @pl.when(jnp.logical_not(itself))
                def _():
                    pltpu.make_async_remote_copy(
                        block,
                        gathered.at[channel],
                        back_send,
                        back_recv,
                        device_id=device(tx, ty, tz, to_core),
                        device_id_type=MESH,
                    ).start()

                return 0

            lax.fori_loop(0, 8, one, 0)
        return 0

    lax.fori_loop(0, 2, give, 0)

    most = message.at[pl.ds(0, CHIPS - 1)]
    pltpu.make_async_copy(most, most, send_sem).wait()

    @pl.when(core != half)
    def _():
        pltpu.make_async_copy(message.at[0], message.at[0], home_sem).wait()
        pltpu.make_async_copy(blocks, blocks, back_send).wait()

    @pl.when(core == half)
    def _():
        rest = blocks.at[pl.ds(0, CHIPS - 1)]
        pltpu.make_async_copy(rest, rest, back_send).wait()

    def swapped(group, _):
        swap_of(group).wait_send()
        return 0

    lax.fori_loop(0, 8, swapped, 0)
    pltpu.make_async_copy(gathered, gathered, back_recv).wait()


def exchange(pair_map, mask, weight):
    dma = pltpu.SemaphoreType.DMA
    return pl.pallas_call(
        exchange_kernel,
        name="exchange",
        out_shape=(
            jax.ShapeDtypeStruct((SUB, WIDE, LANES), BF16),
            jax.ShapeDtypeStruct((CHIPS, TILES, SUB, LANES), BF16),
        ),
        in_specs=[VMEM, VMEM, VMEM],
        out_specs=(VMEM, ANY),
        scratch_shapes=[
            pltpu.VMEM((QUARTER * BOTH * SUB, LANES), F32),
            pltpu.VMEM((CHIPS, BOTH, SUB, LANES), BF16),
            pltpu.VMEM((CHIPS, BOTH, SUB, LANES), BF16),
            pltpu.VMEM((HALF, 2 * LANES), BF16),
            pltpu.VMEM((8, HALF, 2 * LANES), BF16),
            pltpu.VMEM((8, HALF, 2 * LANES), BF16),
            pltpu.VMEM((HALF, 2 * HALF), F32),
            pltpu.VMEM((CHIPS, TILES, SUB, LANES), BF16),
            dma,
            dma,
            dma((8,)),
            dma((8,)),
            dma((8,)),
            dma,
            dma,
        ],
        compiler_params=pltpu.CompilerParams(
            vmem_limit_bytes=BIG, has_side_effects=True, collective_id=0
        ),
    )(pair_map, mask, weight)


def finish_kernel(gathered, normed_ref, gate_weight, out_weight, out_ref, wide, update):
    def widen(channel, _):
        for tile in range(TILES):
            start = pl.multiple_of((channel * TILES + tile) * SUB, SUB)
            wide[pl.ds(start, SUB), :] = gathered[channel, tile].astype(F32)
        return 0

    lax.fori_loop(0, CHIPS, widen, 0)

    def rows_of(sub, _):
        for tile in range(TILES):
            values = wide[pl.ds(tile * SUB + sub, CHIPS, stride=TILES * SUB), :]
            normed_tri = layer_norm(values, 0).astype(BF16)
            mixed = lax.dot_general(
                normed_tri, out_weight[...], (((0,), (0,)), ((), ())), preferred_element_type=F32
            )
            gate = jax.nn.sigmoid(
                jnp.dot(
                    normed_ref[sub, pl.ds(tile * LANES, LANES), :],
                    gate_weight[...],
                    preferred_element_type=F32,
                )
            )
            update[pl.ds(tile * LANES, LANES), :] = (gate * mixed).astype(BF16)
        for seg in range(SEGS):
            out_ref[SUB * seg + sub] = update[pl.ds(seg * BLOCK, BLOCK), :]
        return 0

    lax.fori_loop(0, SUB, rows_of, 0)


def finish(gathered, normed, gate_weight, out_weight):
    return pl.pallas_call(
        finish_kernel,
        name="finish",
        out_shape=jax.ShapeDtypeStruct((BLOCK, BLOCK, LANES), BF16),
        in_specs=[VMEM] * 4,
        out_specs=VMEM,
        scratch_shapes=[
            pltpu.VMEM((CHIPS * TILES * SUB, LANES), F32),
            pltpu.VMEM((WIDE, LANES), BF16),
        ],
        compiler_params=pltpu.CompilerParams(vmem_limit_bytes=BIG),
    )(gathered, normed, gate_weight, out_weight)


def local(pair_map, residue_mask, proj_weight, gate_weight, out_weight):
    mask_float = residue_mask.astype(F32)
    row_mask = lax.dynamic_slice_in_dim(mask_float, lax.axis_index("gx") * BLOCK, BLOCK)
    col = lax.axis_index("gy") * lax.axis_size("gz") + lax.axis_index("gz")
    col_mask = lax.dynamic_slice_in_dim(mask_float, col * BLOCK, BLOCK)
    mask = row_mask.reshape(SEGS, SUB).T[:, :, None] * col_mask[None, None, :]
    mask = mask.reshape(SUB, 1, FLAT)
    mask = jnp.pad(jnp.concatenate([mask, mask], axis=2), ((0, 0), (0, 0), (0, BOTH * LANES - 2 * FLAT)))
    weight = proj_weight.T.reshape(2, 2, 4, QUARTER, LANES).transpose(2, 0, 1, 3, 4)
    weight = weight.reshape(4, 2, 2 * QUARTER, LANES)
    normed, gathered = exchange(pair_map, mask, weight)
    return finish(gathered, normed, gate_weight, out_weight)


def solution(mesh):
    placed = (P("gx", ("gy", "gz"), None), P(), P(), P(), P())
    return jax.shard_map(
        local, mesh=mesh, in_specs=placed, out_specs=P("gx", ("gy", "gz"), None), check_vma=False
    )
```

time: 547 us -> 160 us (0.29)
  waiting for transfers between devices: 273 us -> 0 us
  Pallas kernels: 0 us -> 156 us
  starting transfers between devices: 106 us -> 0 us
  local copies, waits for them, and re-layouts: 62.6 us -> 2.21 us
  blocking collectives: 42 us -> 0 us
  other arithmetic: 38.1 us -> 1.48 us
  matrix products: 22.8 us -> 0 us
    ppermute x6 -> x0, waiting for transfers between devices: 220 us -> none  [partner_2(): lax.ppermute(x, axis, [(i, i ^ 1 << bit) for i in range(lax.axis_size(axi...]
    pallas_call x0 -> x2, Pallas kernels: none -> 156 us  [the longest x1 148 us: exchange(): pl.pallas_call(exchange_kernel, name='exchange', out_shape=(jax.ShapeDtyp...]
    ppermute x6 -> x0, starting transfers between devices: 90.8 us -> none  [partner_2(): lax.ppermute(x, axis, [(i, i ^ 1 << bit) for i in range(lax.axis_size(axi...]
    all_to_all x2 -> x0, waiting for transfers between devices: 53.2 us -> none  [the longest x1 29.7 us: local(): lax.all_to_all(block_tile, ('gy', 'gz'), split_axis=2, concat_axis=0, til...]
    all_to_all x1 -> x0, blocking collectives: 42 us -> none  [local(): lax.all_to_all(left_proj, ('gy', 'gz'), split_axis=0, concat_axis=2, tile...]
    dot_general x4 -> x0, matrix products: 22.8 us -> none  [the longest x1 13 us: local(): jnp.einsum('cik,cjk->cij', left_tile, right_tile, preferred_element_type=...]
    all_to_all x5 -> x0, local copies, waits for them, and re-layouts: 20.9 us -> none  [the longest x2 10.1 us: local(): lax.all_to_all(left_proj, ('gy', 'gz'), split_axis=0, concat_axis=2, tile...]
    convert_element_type x3 -> x0, local copies, waits for them, and re-layouts: 17 us -> none  [whole_channels(): gathered.astype(jnp.float32)]
  transfers between devices with their start and end apart: 8 -> 0, of which waited for: 7 -> 0; matrix products, arithmetic and copies ran while one was open for 4% -> 0% of each run, Pallas kernels for 0% -> 0%
where the time goes in v2:
time: 160 us
  Pallas kernels  156 us (98%)
  local copies, waits for them, and re-layouts  2.21 us (1%)
    pallas_call x1, Pallas kernels, exchange(): pl.pallas_call(exchange_kernel, name='exchange', out_shape=(jax.ShapeDtyp...  148 us
    pallas_call x1, Pallas kernels, finish(): pl.pallas_call(finish_kernel, name='finish', out_shape=jax.ShapeDtypeStru...  7.44 us

profile of v2, /device:TPU:1, one launch (start us, length us, event | category | flops | bytes accessed | tf_op | source)
XLA Modules:
  0.0 159.5 jit_solution(5296017373245087614)
XLA Ops:
  0.0 0.7 convert_element_type.5
  0.7 0.1 fusion.1
  0.8 0.1 mul.41
  0.9 0.1 reshape.46
  0.9 0.1 copy.12
  1.0 0.1 mul.36
  1.1 0.1 mul.44
  1.3 0.8 fusion.mask_ref
  2.0 1.0 copy.15
  3.0 0.7 copy.16
  3.7 148.4 %exchange.1 = (bf16[8,896,128]{2,1,0:T(8,128)(2,1)}, bf16[128,7,8,128]{3,2,1,0:T(8,128)(2,1)}) custom-call(bf16[80,80,128]{2,1,0:T(8,128)(2,1)} %pair_ref.1, f32[8,1,1664]{2,1,0:T(1,128)} %fusion.mask_ref, bf16[4,2,64,128]{3,2,1,0:T(8,128)(2,1)} %bitcast.7), custom_call_target="tpu_custom_call" | custom-call | tf_op jit(solution)/shard_map/exchange/pallas_call | solution.py:323
  152.1 7.4 %finish.1 = bf16[80,80,128]{2,1,0:T(8,128)(2,1)} custom-call(bf16[128,7,8,128]{3,2,1,0:T(8,128)(2,1)} %get-tuple-element.7.gathered, bf16[8,896,128]{2,1,0:T(8,128)(2,1)} %get-tuple-element.8.normed_ref, bf16[128,128]{1,0:T(8,128)(2,1)} %gate_weight.1, bf16[128,128]{1,0:T(8,128)(2,1)} %out_weight.1), custom_call_target="tpu_custom_call" | custom-call | tf_op jit(solution)/shard_map/finish/pallas_call | solution.py:387
  (2 shorter events, 0.0 us)

commit v3 on v2

v3 whole, which is shorter than its diff:
```python
import functools

import jax
import jax.numpy as jnp
from jax import lax
from jax.experimental import pallas as pl
from jax.experimental.pallas import tpu as pltpu
from jax.sharding import PartitionSpec as P

MESH = pl.DeviceIdType.MESH
EPS = 1.0
LANES = 128
BLOCK = 80
FOLD = 4
SUB = 8
SEGS = BLOCK // SUB
TILES = -(-SEGS * BLOCK // LANES)
WIDE = TILES * LANES
EARLY = 5
FLAT = SEGS * BLOCK
BOTH = -(-2 * FLAT // LANES)
EDGE, SPLIT = divmod(FLAT, LANES)
CHIPS = 128
QUARTER = 32
HALF = 640
BF16 = jnp.bfloat16
F32 = jnp.float32
VMEM = pl.BlockSpec(memory_space=pltpu.VMEM)
HBM = pl.BlockSpec(memory_space=pltpu.HBM)
SMEM = pl.BlockSpec(memory_space=pltpu.SMEM)
BIG = 62 * 2**20


def place():
    gx, gy, gz = lax.axis_index("gx"), lax.axis_index("gy"), lax.axis_index("gz")
    return gy, (gz // 2) * 2 + gx % 2, gx // 2, gz % 2


def device(x, y, z, core):
    return (z * 2 + y % 2, x, (y // 2) * 2 + core)


def layer_norm(values, axis):
    average = jnp.mean(values, axis=axis, keepdims=True)
    centred = values - average
    variance = jnp.mean(centred * centred, axis=axis, keepdims=True)
    return centred * lax.rsqrt(variance + EPS)


def lane_index():
    return lax.broadcasted_iota(jnp.int32, (SUB, LANES), 1)


def turn(tile, shift):
    shift %= LANES
    return pltpu.roll(tile, shift, 1) if shift else tile


def unpack_into(tiles, start, target, row, column):
    lanes = lane_index()
    pieces = []
    for seg in range(SEGS):
        first, offset = divmod(start + seg * BLOCK, LANES)
        piece = turn(tiles(first), -offset)
        if offset + BLOCK > LANES:
            piece = jnp.where(lanes < LANES - offset, piece, turn(tiles(first + 1), -offset))
        pieces.append(jnp.where(lanes < BLOCK, piece, 0.0))
    for pair in range(SEGS // 2):
        both = jnp.concatenate(pieces[2 * pair : 2 * pair + 2], axis=0).astype(BF16)
        target[pl.ds(pl.multiple_of(row + 16 * pair, 16), 16), column] = both


def triangle_kernel(
    pair_ref,
    residue_ref,
    proj_ref,
    gate_ref,
    out_weight_ref,
    update_ref,
    raw,
    weight,
    col_mask,
    normed,
    masked,
    gate,
    wide,
    message,
    arrived,
    left,
    right,
    other,
    total,
    early,
    late,
    early_in,
    late_in,
    spread,
    update,
    fetch_sem,
    send_sem,
    home_sem,
    recv_sem,
    swap_send,
    swap_recv,
    back_send,
    back_recv,
):
    x, y, z, core = place()
    half = y % 2
    gx, gy, gz = lax.axis_index("gx"), lax.axis_index("gy"), lax.axis_index("gz")
    barrier = pltpu.get_barrier_semaphore()
    dot = functools.partial(lax.dot_general, preferred_element_type=F32)

    fetch = pltpu.make_async_copy(pair_ref, raw, fetch_sem)
    fetch.start()

    with jax.named_scope("greet"):
        seats_x = [lax.rem(x + n, 4) * 4 for n in range(4)]
        seats_y = [lax.rem(y // 2 + n, 2) * 2 for n in range(2)]
        seats_z = [lax.rem(z + n, 8) * 32 + core * 16 for n in range(8)]
        seats_core = [core, 1 - core]
        for at_z in range(8):
            for at_x in range(4):
                for at_y in range(2):
                    for at_core in range(2):
                        seat = seats_z[at_z] + seats_x[at_x] + seats_y[at_y] + seats_core[at_core]
                        hello = functools.partial(
                            pl.semaphore_signal,
                            barrier,
                            inc=1,
                            device_id=seat,
                            device_id_type=pl.DeviceIdType.LOGICAL,
                        )
                        if at_z or at_x or at_y or at_core:
                            hello()
                        else:
                            pl.when(core != half)(hello)

    with jax.named_scope("masks"):
        for row in range(BLOCK):
            value = residue_ref[(gy * 4 + gz) * BLOCK + row].astype(F32)
            col_mask[pl.ds(row, 1), :] = jnp.full((1, LANES), value)
    mean_of = jnp.full((LANES, LANES), 1.0 / LANES, BF16)

    with jax.named_scope("turn"):
        turned = proj_ref[...].T
        for to_y in range(4):
            for kind in range(4):
                start = kind * LANES + to_y * QUARTER
                target = pl.ds(kind % 2 * QUARTER, QUARTER)
                weight[to_y, kind // 2, target, :] = turned[start : start + QUARTER]
    fetch.wait()

    def norm_rows(sub):
        for seg in range(SEGS):
            row = SUB * seg + sub
            rows = raw[row]
            values = rows.astype(F32)
            average = dot(rows, mean_of, (((1,), (0,)), ((), ())))
            square = jnp.mean(values * values, axis=1, keepdims=True)
            result = (values - average) * lax.rsqrt(square - average * average + EPS)
            normed[sub, pl.ds(seg * BLOCK, BLOCK), :] = result.astype(BF16)
            keep = col_mask[...] * residue_ref[gx * BLOCK + row].astype(F32)
            masked[sub, pl.ds(seg * BLOCK, BLOCK), :] = (result * keep).astype(BF16)
        rest = pl.ds(FLAT, WIDE - FLAT)
        normed[sub, rest, :] = jnp.zeros((WIDE - FLAT, LANES), BF16)
        masked[sub, rest, :] = jnp.zeros((WIDE - FLAT, LANES), BF16)

    def project(sub, to_y):
        if True:
            for tile in range(BOTH):
                if tile < EDGE:
                    block = masked[sub, pl.ds(tile * LANES, LANES), :]
                elif tile == EDGE:
                    block = jnp.concatenate(
                        [
                            masked[sub, pl.ds(EDGE * LANES, SPLIT), :],
                            masked[sub, pl.ds(0, LANES - SPLIT), :],
                        ],
                        axis=0,
                    )
                else:
                    start = (tile - EDGE) * LANES - SPLIT
                    block = masked[sub, pl.ds(start, LANES), :]
                value = None
                for side in range(2):
                    if (side == 0 and tile > EDGE) or (side == 1 and tile < EDGE):
                        continue
                    projected = lax.dot_general(
                        weight[to_y, side],
                        block,
                        (((1,), (1,)), ((), ())),
                        preferred_element_type=F32,
                    )
                    gated = jax.nn.sigmoid(projected[:QUARTER]) * projected[QUARTER:]
                    if value is None:
                        value = gated
                    else:
                        lanes = lax.broadcasted_iota(jnp.int32, (QUARTER, LANES), 1)
                        value = jnp.where(lanes < SPLIT, value, gated)
                wide[pl.ds(tile * SUB + sub, QUARTER, stride=BOTH * SUB), :] = value

    def pack(to_y):
        def one(number, _):
            for tile in range(BOTH):
                start = pl.multiple_of((number * BOTH + tile) * SUB, SUB)
                message[to_y * QUARTER + number, tile] = wide[pl.ds(start, SUB), :].astype(BF16)
            return 0

        with jax.named_scope("pack"):
            lax.fori_loop(0, QUARTER, one, 0)

    slot = (x * 4 + (y // 2) * 2 + core) * 8 + z

    def send_all(turn_y, to_y, first):
        def send(step, _):
            dz, dx = step % 8, step // 8
            tx, tz = (x + dx) % 4, (z + dz) % 8
            pltpu.make_async_remote_copy(
                message.at[to_y * QUARTER + tz * 4 + tx],
                arrived.at[slot],
                send_sem,
                recv_sem.at[turn_y // 2 * 4 + dx],
                device_id=device(tx, to_y, tz, half),
                device_id_type=MESH,
            ).start()
            return 0

        with jax.named_scope("send"):
            lax.fori_loop(first, QUARTER, send, 0)

    with jax.named_scope("norm"):
        for sub in range(SUB):
            norm_rows(sub)
            project(sub, y)
    pack(y)
    with jax.named_scope("meet"):

        @pl.when(core == half)
        def _():
            pl.semaphore_wait(barrier, CHIPS - 1)

        @pl.when(core != half)
        def _():
            pl.semaphore_wait(barrier, CHIPS)

    own = message.at[y * QUARTER + z * 4 + x]

    @pl.when(core == half)
    def _():
        pltpu.make_async_copy(own, arrived.at[slot], recv_sem.at[0]).start()

    @pl.when(core != half)
    def _():
        pltpu.make_async_remote_copy(
            own,
            arrived.at[slot],
            home_sem,
            recv_sem.at[0],
            device_id=device(x, y, z, half),
            device_id_type=MESH,
        ).start()

    send_all(0, y, 1)

    def quarter(turn_y, _):
        to_y = (y // 2 + turn_y // 2) % 2 * 2 + (y + turn_y) % 2

        def one(sub, _):
            project(sub, to_y)
            return 0

        with jax.named_scope("project"):
            lax.fori_loop(0, SUB, one, 0)
        pack(to_y)
        send_all(turn_y, to_y, 0)
        return 0

    lax.fori_loop(1, 4, quarter, 0)

    def gate_rows(sub, _):
        for tile in range(TILES):
            block = normed[sub, pl.ds(tile * LANES, LANES), :]
            value = dot(block, gate_ref[...], (((1,), (0,)), ((), ())))
            gate[sub, pl.ds(tile * LANES, LANES), :] = jax.nn.sigmoid(value)
        return 0

    with jax.named_scope("gate"):
        lax.fori_loop(0, SUB, gate_rows, 0)

    def clear(step, _):
        total[pl.ds(pl.multiple_of(step * 16, 16), 16), :] = jnp.zeros((16, total.shape[1]), F32)
        return 0

    with jax.named_scope("clear"):
        lax.fori_loop(0, 40, clear, 0)

    def swap_of(group):
        return pltpu.make_async_remote_copy(
            right.at[group],
            other.at[group],
            swap_send.at[group],
            swap_recv.at[group],
            device_id=device(x, y, z, 1 - core),
            device_id_type=MESH,
        )

    def multiply(factor, start):
        total[:, pl.ds(start, HALF)] += lax.dot_general(
            left[...],
            factor[...],
            (((1,), (1,)), ((), ())),
            preferred_element_type=F32,
        )

    def take(group):
        base = ((x - group) % 4 * 4 + (y // 2 + group // 4) % 2 * 2) * 8
        some = arrived.at[pl.ds(0, 16)]
        with jax.named_scope("arrive"):
            pltpu.make_async_copy(some, some, recv_sem.at[group]).wait()

        def unpack(source, start, target, row):
            for side in range(2):

                def tile_of(number, side=side):
                    return arrived[base + side * 8 + source, number].astype(F32)

                unpack_into(tile_of, start, target, row * BLOCK, pl.ds(side * LANES, LANES))

        def unpack_right(row, _):
            seat = lax.rem(row // 2 + 4 - x, 4) * 2 + lax.rem(row + y // 2, 2)
            unpack(row, FLAT, right.at[group], seat)
            return 0

        def unpack_left(row, _):
            unpack(row, 0, left, row)
            return 0

        with jax.named_scope("unpack"):
            lax.fori_loop(0, 8, unpack_right, 0)
        swap_of(group).start()
        with jax.named_scope("unpack"):
            lax.fori_loop(0, 8, unpack_left, 0)
        with jax.named_scope("multiply"):
            multiply(right.at[group], 0)

    def take_other(group):
        with jax.named_scope("swap"):
            swap_of(group).wait_recv()
        with jax.named_scope("multiply"):
            multiply(other.at[group], HALF)

    def take_both(group, _):
        take(group)
        take_other(group)
        return 0

    lax.fori_loop(0, 7, take_both, 0)
    take(7)

    channel = y * QUARTER + z * 4 + x

    def launch(side, seat, dz, part):
        tx, tz = lax.rem(x + seat // 2, 4), lax.rem(z + dz, 8)
        ty, to_core = lax.rem(y // 2 + seat % 2, 2), lax.rem(core + side, 2)
        source = (early, late)[part].at[(side * 8 + seat) * 8 + dz]
        target = (early_in, late_in)[part].at[channel]

        def away():
            pltpu.make_async_remote_copy(
                source,
                target,
                back_send.at[part],
                back_recv.at[part],
                device_id=tz * 32 + core * 16 + tx * 4 + ty * 2 + to_core,
                device_id_type=pl.DeviceIdType.LOGICAL,
            ).start()

        def home():
            pltpu.make_async_copy(source, target, back_recv.at[part]).start()

        if seat or side:
            away()
        else:
            itself = (dz == 0) & (core == half)
            pl.when(itself)(home)
            pl.when(jnp.logical_not(itself))(away)

    def give(side):
        for seat in range(8):

            def one(dz, _, seat=seat):
                tz = lax.rem(z + dz, 8)
                lanes = lane_index()
                tiles = [None] * TILES
                for seg in range(SEGS):
                    row = pl.ds(pl.multiple_of(tz * BLOCK + seg * SUB, SUB), SUB)
                    low, high, done = seat * BLOCK, seg * BLOCK, 0
                    while done < BLOCK:
                        from_tile, from_lane = divmod(low + done, LANES)
                        to_tile, to_lane = divmod(high + done, LANES)
                        start = side * HALF + from_tile * LANES
                        piece = turn(total[row, pl.ds(start, LANES)], to_lane - from_lane)
                        if tiles[to_tile] is None:
                            tiles[to_tile] = piece
                        else:
                            tiles[to_tile] = jnp.where(lanes < to_lane, tiles[to_tile], piece)
                        done += min(BLOCK - done, LANES - from_lane, LANES - to_lane)
                number = (side * 8 + seat) * 8 + dz
                for tile in range(EARLY):
                    early[number, tile] = tiles[tile].astype(BF16)
                launch(side, seat, dz, 0)
                folded = turn(pltpu.roll(tiles[EARLY + 1], FOLD, 0), SPLIT)
                folded = jnp.where(lanes < SPLIT, tiles[EARLY + 1], folded)
                late[number, 0] = tiles[EARLY][:FOLD].astype(BF16)
                late[number, 1] = tiles[EARLY][FOLD:].astype(BF16)
                late[number, 2] = folded[:FOLD].astype(BF16)
                return 0

            with jax.named_scope("give"):
                lax.fori_loop(0, 8, one, 0)

    give(0)
    take_other(7)
    give(1)

    def give_late(dz, _):
        for side in range(2):
            for seat in range(8):
                launch(side, seat, dz, 1)
        return 0

    with jax.named_scope("late"):
        lax.fori_loop(0, 8, give_late, 0)

    def whole(rows, count):
        values = spread[pl.ds(rows, CHIPS, stride=count), :]
        normed_tri = layer_norm(values, 0).astype(BF16)
        return dot(normed_tri, out_weight_ref[...], (((0,), (0,)), ((), ())))

    with jax.named_scope("gather"):
        pltpu.make_async_copy(early_in, early_in, back_recv.at[0]).wait()

    def widen_early(number, _):
        for step in range(2):
            for tile in range(EARLY):
                row = pl.multiple_of(((2 * number + step) * EARLY + tile) * SUB, SUB)
                spread[pl.ds(row, SUB), :] = early_in[2 * number + step, tile].astype(F32)
        return 0

    def finish_early(sub, _):
        for tile in range(EARLY):
            mixed = whole(tile * SUB + sub, EARLY * SUB)
            lanes = pl.ds(tile * LANES, LANES)
            update[sub, lanes, :] = (gate[sub, lanes, :] * mixed).astype(BF16)
        return 0

    with jax.named_scope("widen"):
        lax.fori_loop(0, CHIPS // 2, widen_early, 0)
    with jax.named_scope("finish"):
        lax.fori_loop(0, SUB, finish_early, 0)

    with jax.named_scope("gather"):
        pltpu.make_async_copy(late_in, late_in, back_recv.at[1]).wait()

    def widen_late(number, _):
        for step in range(4):
            for tile in range(3):
                row = pl.multiple_of((4 * number + step) * 16, 16) + tile * FOLD
                spread[pl.ds(row, FOLD), :] = late_in[4 * number + step, tile].astype(F32)
        return 0

    with jax.named_scope("widen"):
        lax.fori_loop(0, CHIPS // 4, widen_late, 0)
    with jax.named_scope("finish"):
        for sub in range(SUB):
            mixed = whole(sub, 16)
            lanes = pl.ds(EARLY * LANES, LANES)
            update[sub, lanes, :] = (gate[sub, lanes, :] * mixed).astype(BF16)
        rest = pl.ds((EARLY + 1) * LANES, SPLIT)
        for sub in range(FOLD):
            mixed = whole(SUB + sub, 16)
            update[sub, rest, :] = (gate[sub, rest, :] * mixed[:SPLIT]).astype(BF16)
            update[FOLD + sub, rest, :] = (
                gate[FOLD + sub, rest, :] * mixed[SPLIT : 2 * SPLIT]
            ).astype(BF16)

    def settle(sub, _):
        for seg in range(SEGS):
            update_ref[SUB * seg + sub] = update[sub, pl.ds(seg * BLOCK, BLOCK), :]
        return 0

    with jax.named_scope("settle"):
        lax.fori_loop(0, SUB, settle, 0)
        most = message.at[pl.ds(0, CHIPS - 1)]
        pltpu.make_async_copy(most, most, send_sem).wait()

    for part, source in enumerate((early, late)):

        @pl.when(core != half)
        def _():
            pltpu.make_async_copy(source, source, back_send.at[part]).wait()

        @pl.when(core == half)
        def _():
            rest = source.at[pl.ds(0, CHIPS - 1)]
            pltpu.make_async_copy(rest, rest, back_send.at[part]).wait()

    @pl.when(core != half)
    def _():
        pltpu.make_async_copy(message.at[0], message.at[0], home_sem).wait()

    def swapped(group, _):
        swap_of(group).wait_send()
        return 0

    lax.fori_loop(0, 8, swapped, 0)


def local(pair_map, residue_mask, proj_weight, gate_weight, out_weight):
    dma = pltpu.SemaphoreType.DMA
    return pl.pallas_call(
        triangle_kernel,
        name="triangle",
        out_shape=jax.ShapeDtypeStruct(pair_map.shape, BF16),
        in_specs=[HBM, SMEM, VMEM, VMEM, VMEM],
        out_specs=VMEM,
        scratch_shapes=[
            pltpu.VMEM((BLOCK, BLOCK, LANES), BF16),
            pltpu.VMEM((4, 2, 2 * QUARTER, LANES), BF16),
            pltpu.VMEM((BLOCK, LANES), F32),
            pltpu.VMEM((SUB, WIDE, LANES), BF16),
            pltpu.VMEM((SUB, WIDE, LANES), BF16),
            pltpu.VMEM((SUB, WIDE, LANES), F32),
            pltpu.VMEM((QUARTER * BOTH * SUB, LANES), F32),
            pltpu.VMEM((CHIPS, BOTH, SUB, LANES), BF16),
            pltpu.VMEM((CHIPS, BOTH, SUB, LANES), BF16),
            pltpu.VMEM((HALF, 2 * LANES), BF16),
            pltpu.VMEM((8, HALF, 2 * LANES), BF16),
            pltpu.VMEM((8, HALF, 2 * LANES), BF16),
            pltpu.VMEM((HALF, 2 * HALF), F32),
            pltpu.VMEM((CHIPS, EARLY, SUB, LANES), BF16),
            pltpu.VMEM((CHIPS, 3, FOLD, LANES), BF16),
            pltpu.VMEM((CHIPS, EARLY, SUB, LANES), BF16),
            pltpu.VMEM((CHIPS, 3, FOLD, LANES), BF16),
            pltpu.VMEM((CHIPS * EARLY * SUB, LANES), F32),
            pltpu.VMEM((SUB, WIDE, LANES), BF16),
            dma,
            dma,
            dma,
            dma((8,)),
            dma((8,)),
            dma((8,)),
            dma((2,)),
            dma((2,)),
        ],
        compiler_params=pltpu.CompilerParams(
            vmem_limit_bytes=BIG, has_side_effects=True, collective_id=0
        ),
    )(pair_map, residue_mask, proj_weight, gate_weight, out_weight)


def solution(mesh):
    placed = (P("gx", ("gy", "gz"), None), P(), P(), P(), P())
    return jax.shard_map(
        local, mesh=mesh, in_specs=placed, out_specs=P("gx", ("gy", "gz"), None), check_vma=False
    )
```

time: 160 us -> 142 us (0.89)
  Pallas kernels: 156 us -> 139 us
    pallas_call x2 -> x1, Pallas kernels: 156 us -> 139 us  [local(): pl.pallas_call(triangle_kernel, name='triangle', out_shape=jax.ShapeDtype...]
    unnamed x1, local copies, waits for them, and re-layouts: 1.02 us -> 2.7 us
where the time goes in v3:
time: 142 us
  Pallas kernels  139 us (98%)
  local copies, waits for them, and re-layouts  2.7 us (2%)
    pallas_call x1, Pallas kernels, local(): pl.pallas_call(triangle_kernel, name='triangle', out_shape=jax.ShapeDtype...  139 us

profile of v3, /device:TPU:1, one launch (start us, length us, event | category | flops | bytes accessed | tf_op | source)
XLA Modules:
  0.0 141.9 jit_solution(4131856296410539134)
XLA Ops:
  0.0 139.2 %triangle.1 = bf16[80,80,128]{2,1,0:T(8,128)(2,1)} custom-call(bf16[80,80,128]{2,1,0:T(8,128)(2,1)} %pair_ref.1, s32[1280]{0:T(1024)} %residue_ref.1, bf16[128,512]{1,0:T(8,128)(2,1)} %proj_ref.1, bf16[128,128]{1,0:T(8,128)(2,1)} %gate_ref.1, bf16[128,128]{1,0:T(8,128)(2,1)} %out_weight_ref.1), custom_call_target="tpu_custom_call" | custom-call | tf_op jit(solution)/shard_map/triangle/pallas_call | solution.py:522
  139.2 2.7 %copy.7 = bf16[80,80,128]{2,1,0:T(8,128)(2,1)} copy(bf16[80,80,128]{2,1,0:T(8,128)(2,1)} %triangle.1) | data formatting | bytes 3276800

commit v4 on v3

--- a/solution.py
+++ b/solution.py
@@ -19,6 +19,7 @@
 EARLY = 5
 FLAT = SEGS * BLOCK
 BOTH = -(-2 * FLAT // LANES)
+PACKED = 2 * FLAT * SUB // (FOLD * LANES)
 EDGE, SPLIT = divmod(FLAT, LANES)
 CHIPS = 128
 QUARTER = 32
@@ -27,8 +28,7 @@
 F32 = jnp.float32
 VMEM = pl.BlockSpec(memory_space=pltpu.VMEM)
 HBM = pl.BlockSpec(memory_space=pltpu.HBM)
-SMEM = pl.BlockSpec(memory_space=pltpu.SMEM)
-BIG = 62 * 2**20
+BIG = 46 * 2**20
 
 
 def place():
@@ -71,12 +71,16 @@
 
 
 def triangle_kernel(
-    pair_ref,
+    pair_hbm,
+    residue_hbm,
+    proj_hbm,
+    gate_hbm,
+    out_weight_hbm,
+    update_ref,
     residue_ref,
     proj_ref,
     gate_ref,
     out_weight_ref,
-    update_ref,
     raw,
     weight,
     col_mask,
@@ -111,8 +115,20 @@
     barrier = pltpu.get_barrier_semaphore()
     dot = functools.partial(lax.dot_general, preferred_element_type=F32)
 
-    fetch = pltpu.make_async_copy(pair_ref, raw, fetch_sem)
-    fetch.start()
+    fetches = [
+        pltpu.make_async_copy(source, target, fetch_sem.at[number])
+        for number, (source, target) in enumerate(
+            (
+                (pair_hbm, raw),
+                (residue_hbm, residue_ref),
+                (proj_hbm, proj_ref),
+                (gate_hbm, gate_ref),
+                (out_weight_hbm, out_weight_ref),
+            )
+        )
+    ]
+    for fetch in fetches:
+        fetch.start()
 
     with jax.named_scope("greet"):
         seats_x = [lax.rem(x + n, 4) * 4 for n in range(4)]
@@ -136,6 +152,8 @@
                         else:
                             pl.when(core != half)(hello)
 
+    for fetch in fetches[1:]:
+        fetch.wait()
     with jax.named_scope("masks"):
         for row in range(BLOCK):
             value = residue_ref[(gy * 4 + gz) * BLOCK + row].astype(F32)
@@ -149,7 +167,7 @@
                 start = kind * LANES + to_y * QUARTER
                 target = pl.ds(kind % 2 * QUARTER, QUARTER)
                 weight[to_y, kind // 2, target, :] = turned[start : start + QUARTER]
-    fetch.wait()
+    fetches[0].wait()
 
     def norm_rows(sub):
         for seg in range(SEGS):
@@ -202,9 +220,15 @@
 
     def pack(to_y):
         def one(number, _):
-            for tile in range(BOTH):
+            to = to_y * QUARTER + number
+            for tile in range(BOTH - 1):
                 start = pl.multiple_of((number * BOTH + tile) * SUB, SUB)
-                message[to_y * QUARTER + number, tile] = wide[pl.ds(start, SUB), :].astype(BF16)
+                message[to, 2 * tile] = wide[pl.ds(start, FOLD), :].astype(BF16)
+                message[to, 2 * tile + 1] = wide[pl.ds(start + FOLD, FOLD), :].astype(BF16)
+            last = wide[pl.ds(pl.multiple_of((number * BOTH + BOTH - 1) * SUB, SUB), SUB), :]
+            folded = turn(pltpu.roll(last, FOLD, 0), LANES // 2)
+            folded = jnp.where(lane_index() < LANES // 2, last, folded)
+            message[to, PACKED - 1] = folded[:FOLD].astype(BF16)
             return 0
 
         with jax.named_scope("pack"):
@@ -322,8 +346,18 @@
         def unpack(source, start, target, row):
             for side in range(2):
 
-                def tile_of(number, side=side):
-                    return arrived[base + side * 8 + source, number].astype(F32)
+                cache = {}
+
+                def tile_of(number, side=side, cache=cache):
+                    if number not in cache:
+                        at = base + side * 8 + source
+                        upper = arrived[at, 2 * number].astype(F32)
+                        if number < BOTH - 1:
+                            lower = arrived[at, 2 * number + 1].astype(F32)
+                        else:
+                            lower = turn(upper, LANES // 2)
+                        cache[number] = jnp.concatenate([upper, lower], axis=0)
+                    return cache[number]
 
                 unpack_into(tile_of, start, target, row * BLOCK, pl.ds(side * LANES, LANES))
 
@@ -519,13 +553,21 @@
 
 def local(pair_map, residue_mask, proj_weight, gate_weight, out_weight):
     dma = pltpu.SemaphoreType.DMA
+    inputs = [
+        pltpu.with_memory_space_constraint(array, pltpu.HBM)
+        for array in (pair_map, residue_mask, proj_weight, gate_weight, out_weight)
+    ]
     return pl.pallas_call(
         triangle_kernel,
         name="triangle",
         out_shape=jax.ShapeDtypeStruct(pair_map.shape, BF16),
-        in_specs=[HBM, SMEM, VMEM, VMEM, VMEM],
+        in_specs=[HBM] * 5,
         out_specs=VMEM,
         scratch_shapes=[
+            pltpu.SMEM(residue_mask.shape, jnp.int32),
+            pltpu.VMEM(proj_weight.shape, BF16),
+            pltpu.VMEM(gate_weight.shape, BF16),
+            pltpu.VMEM(out_weight.shape, BF16),
             pltpu.VMEM((BLOCK, BLOCK, LANES), BF16),
             pltpu.VMEM((4, 2, 2 * QUARTER, LANES), BF16),
             pltpu.VMEM((BLOCK, LANES), F32),
@@ -533,8 +575,8 @@
             pltpu.VMEM((SUB, WIDE, LANES), BF16),
             pltpu.VMEM((SUB, WIDE, LANES), F32),
             pltpu.VMEM((QUARTER * BOTH * SUB, LANES), F32),
-            pltpu.VMEM((CHIPS, BOTH, SUB, LANES), BF16),
-            pltpu.VMEM((CHIPS, BOTH, SUB, LANES), BF16),
+            pltpu.VMEM((CHIPS, PACKED, FOLD, LANES), BF16),
+            pltpu.VMEM((CHIPS, PACKED, FOLD, LANES), BF16),
             pltpu.VMEM((HALF, 2 * LANES), BF16),
             pltpu.VMEM((8, HALF, 2 * LANES), BF16),
             pltpu.VMEM((8, HALF, 2 * LANES), BF16),
@@ -545,7 +587,7 @@
             pltpu.VMEM((CHIPS, 3, FOLD, LANES), BF16),
             pltpu.VMEM((CHIPS * EARLY * SUB, LANES), F32),
             pltpu.VMEM((SUB, WIDE, LANES), BF16),
-            dma,
+            dma((5,)),
             dma,
             dma,
             dma((8,)),
@@ -557,7 +599,7 @@
         compiler_params=pltpu.CompilerParams(
             vmem_limit_bytes=BIG, has_side_effects=True, collective_id=0
         ),
-    )(pair_map, residue_mask, proj_weight, gate_weight, out_weight)
+    )(*inputs)
 
 
 def solution(mesh):

time: 142 us -> 135 us (0.951)
  Pallas kernels: 139 us -> 134 us
  local copies, waits for them, and re-layouts: 2.7 us -> 1.17 us
    pallas_call x1, Pallas kernels: 139 us -> 134 us  [local(): pl.pallas_call(triangle_kernel, name='triangle', out_shape=jax.ShapeDtype...]
    unnamed x1, local copies, waits for them, and re-layouts: 2.7 us -> 1.17 us
where the time goes in v4:
time: 135 us
  Pallas kernels  134 us (99%)
    pallas_call x1, Pallas kernels, local(): pl.pallas_call(triangle_kernel, name='triangle', out_shape=jax.ShapeDtype...  134 us

profile of v4, /device:TPU:1, one launch (start us, length us, event | category | flops | bytes accessed | tf_op | source)
XLA Modules:
  0.0 135.3 jit_solution(10977805546784118318)
XLA Ops:
  0.0 134.2 %triangle.1 = bf16[80,80,128]{2,1,0:T(8,128)(2,1)S(1)} custom-call(bf16[80,80,128]{2,1,0:T(8,128)(2,1)} %pair_hbm.1, s32[1280]{0:T(1024)} %residue_hbm.1, bf16[128,512]{1,0:T(8,128)(2,1)} %proj_hbm.1, bf16[128,128]{1,0:T(8,128)(2,1)} %gate_hbm.1, bf16[128,128]{1,0:T(8,128)(2,1)} %out_weight_hbm.1), custom_call_target="tpu_custom_call" | custom-call | tf_op jit(solution)/shard_map/triangle/pallas_call | solution.py:560
  134.2 1.2 copy.7

commit v5 on v4

--- a/solution.py
+++ b/solution.py
@@ -219,7 +219,7 @@
                 wide[pl.ds(tile * SUB + sub, QUARTER, stride=BOTH * SUB), :] = value
 
     def pack(to_y):
-        def one(number, _):
+        def pack_one(number):
             to = to_y * QUARTER + number
             for tile in range(BOTH - 1):
                 start = pl.multiple_of((number * BOTH + tile) * SUB, SUB)
@@ -229,10 +229,14 @@
             folded = turn(pltpu.roll(last, FOLD, 0), LANES // 2)
             folded = jnp.where(lane_index() < LANES // 2, last, folded)
             message[to, PACKED - 1] = folded[:FOLD].astype(BF16)
+
+        def one(step, _):
+            for number in range(8):
+                pack_one(8 * step + number)
             return 0
 
         with jax.named_scope("pack"):
-            lax.fori_loop(0, QUARTER, one, 0)
+            lax.fori_loop(0, QUARTER // 8, one, 0)
 
     slot = (x * 4 + (y // 2) * 2 + core) * 8 + z
 
@@ -329,9 +333,9 @@
             device_id_type=MESH,
         )
 
-    def multiply(factor, start):
+    def multiply(group, factor, start):
         total[:, pl.ds(start, HALF)] += lax.dot_general(
-            left[...],
+            left[group],
             factor[...],
             (((1,), (1,)), ((), ())),
             preferred_element_type=F32,
@@ -361,35 +365,37 @@
 
                 unpack_into(tile_of, start, target, row * BLOCK, pl.ds(side * LANES, LANES))
 
-        def unpack_right(row, _):
-            seat = lax.rem(row // 2 + 4 - x, 4) * 2 + lax.rem(row + y // 2, 2)
-            unpack(row, FLAT, right.at[group], seat)
+        def unpack_right(step, _):
+            for low in range(2):
+                seat = lax.rem(step + 4 - x, 4) * 2 + lax.rem(low + y // 2, 2)
+                unpack(2 * step + low, FLAT, right.at[group], seat)
             return 0
 
-        def unpack_left(row, _):
-            unpack(row, 0, left, row)
+        def unpack_left(step, _):
+            for low in range(2):
+                unpack(2 * step + low, 0, left.at[group], 2 * step + low)
             return 0
 
         with jax.named_scope("unpack"):
-            lax.fori_loop(0, 8, unpack_right, 0)
+            lax.fori_loop(0, 4, unpack_right, 0)
         swap_of(group).start()
         with jax.named_scope("unpack"):
-            lax.fori_loop(0, 8, unpack_left, 0)
+            lax.fori_loop(0, 4, unpack_left, 0)
         with jax.named_scope("multiply"):
-            multiply(right.at[group], 0)
+            multiply(group, right.at[group], 0)
 
     def take_other(group):
         with jax.named_scope("swap"):
             swap_of(group).wait_recv()
         with jax.named_scope("multiply"):
-            multiply(other.at[group], HALF)
-
-    def take_both(group, _):
+            multiply(group, other.at[group], HALF)
+
+    def take_own(group, _):
         take(group)
-        take_other(group)
-        return 0
-
-    lax.fori_loop(0, 7, take_both, 0)
+        pl.when(core != half)(lambda: take_other(group))
+        return 0
+
+    lax.fori_loop(0, 7, take_own, 0)
     take(7)
 
     channel = y * QUARTER + z * 4 + x
@@ -455,6 +461,15 @@
                 lax.fori_loop(0, 8, one, 0)
 
     give(0)
+
+    @pl.when(core == half)
+    def _():
+        def rest(group, _):
+            take_other(group)
+            return 0
+
+        lax.fori_loop(0, 7, rest, 0)
+
     take_other(7)
     give(1)
 
@@ -577,7 +592,7 @@
             pltpu.VMEM((QUARTER * BOTH * SUB, LANES), F32),
             pltpu.VMEM((CHIPS, PACKED, FOLD, LANES), BF16),
             pltpu.VMEM((CHIPS, PACKED, FOLD, LANES), BF16),
-            pltpu.VMEM((HALF, 2 * LANES), BF16),
+            pltpu.VMEM((8, HALF, 2 * LANES), BF16),
             pltpu.VMEM((8, HALF, 2 * LANES), BF16),
             pltpu.VMEM((8, HALF, 2 * LANES), BF16),
             pltpu.VMEM((HALF, 2 * HALF), F32),

time: 135 us -> 129 us (0.956)
  Pallas kernels: 134 us -> 128 us
    pallas_call x1, Pallas kernels: 134 us -> 128 us  [local(): pl.pallas_call(triangle_kernel, name='triangle', out_shape=jax.ShapeDtype...]
where the time goes in v5:
time: 129 us
  Pallas kernels  128 us (99%)
    pallas_call x1, Pallas kernels, local(): pl.pallas_call(triangle_kernel, name='triangle', out_shape=jax.ShapeDtype...  128 us

profile of v5, /device:TPU:1, one launch (start us, length us, event | category | flops | bytes accessed | tf_op | source)
XLA Modules:
  0.0 129.1 jit_solution(2257037486476487601)
XLA Ops:
  0.0 127.9 %triangle.1 = bf16[80,80,128]{2,1,0:T(8,128)(2,1)S(1)} custom-call(bf16[80,80,128]{2,1,0:T(8,128)(2,1)} %pair_hbm.1, s32[1280]{0:T(1024)} %residue_hbm.1, bf16[128,512]{1,0:T(8,128)(2,1)} %proj_hbm.1, bf16[128,128]{1,0:T(8,128)(2,1)} %gate_hbm.1, bf16[128,128]{1,0:T(8,128)(2,1)} %out_weight_hbm.1), custom_call_target="tpu_custom_call" | custom-call | tf_op jit(solution)/shard_map/triangle/pallas_call | solution.py:575
  127.9 1.2 copy.7

commit v6 on v5

--- a/solution.py
+++ b/solution.py
@@ -38,6 +38,11 @@
 
 def device(x, y, z, core):
     return (z * 2 + y % 2, x, (y // 2) * 2 + core)
+
+
+def far_first(step):
+    half = (step + 1) // 2
+    return 4 + half * (1 - 2 * lax.rem(step, 2))
 
 
 def layer_norm(values, axis):
@@ -240,10 +245,12 @@
 
     slot = (x * 4 + (y // 2) * 2 + core) * 8 + z
 
-    def send_all(turn_y, to_y, first):
+    def send_all(turn_y, to_y, first, order):
         def send(step, _):
-            dz, dx = step % 8, step // 8
-            tx, tz = (x + dx) % 4, (z + dz) % 8
+            dz, dx = lax.rem(step, 8), step // 8
+            if order:
+                dz = order(dz)
+            tx, tz = lax.rem(x + dx, 4), lax.rem(z + dz, 8)
             pltpu.make_async_remote_copy(
                 message.at[to_y * QUARTER + tz * 4 + tx],
                 arrived.at[slot],
@@ -289,7 +296,7 @@
             device_id_type=MESH,
         ).start()
 
-    send_all(0, y, 1)
+    send_all(0, y, 1, None)
 
     def quarter(turn_y, _):
         to_y = (y // 2 + turn_y // 2) % 2 * 2 + (y + turn_y) % 2
@@ -301,7 +308,7 @@
         with jax.named_scope("project"):
             lax.fori_loop(0, SUB, one, 0)
         pack(to_y)
-        send_all(turn_y, to_y, 0)
+        send_all(turn_y, to_y, 0, far_first)
         return 0
 
     lax.fori_loop(1, 4, quarter, 0)
@@ -429,7 +436,8 @@
     def give(side):
         for seat in range(8):
 
-            def one(dz, _, seat=seat):
+            def one(step, _, seat=seat):
+                dz = far_first(step)
                 tz = lax.rem(z + dz, 8)
                 lanes = lane_index()
                 tiles = [None] * TILES
@@ -473,7 +481,8 @@
     take_other(7)
     give(1)
 
-    def give_late(dz, _):
+    def give_late(step, _):
+        dz = far_first(step)
         for side in range(2):
             for seat in range(8):
                 launch(side, seat, dz, 1)

time: 129 us -> 128 us (level)
    pallas_call x1, Pallas kernels: 128 us -> 127 us  [local(): pl.pallas_call(triangle_kernel, name='triangle', out_shape=jax.ShapeDtype...]
where the time goes in v6:
time: 128 us
  Pallas kernels  127 us (99%)
    pallas_call x1, Pallas kernels, local(): pl.pallas_call(triangle_kernel, name='triangle', out_shape=jax.ShapeDtype...  127 us

profile of v6, /device:TPU:1, one launch (start us, length us, event | category | flops | bytes accessed | tf_op | source)
XLA Modules:
  0.0 127.8 jit_solution(13823034780066031479)
XLA Ops:
  0.0 126.6 %triangle.1 = bf16[80,80,128]{2,1,0:T(8,128)(2,1)S(1)} custom-call(bf16[80,80,128]{2,1,0:T(8,128)(2,1)} %pair_hbm.1, s32[1280]{0:T(1024)} %residue_hbm.1, bf16[128,512]{1,0:T(8,128)(2,1)} %proj_hbm.1, bf16[128,128]{1,0:T(8,128)(2,1)} %gate_hbm.1, bf16[128,128]{1,0:T(8,128)(2,1)} %out_weight_hbm.1), custom_call_target="tpu_custom_call" | custom-call | tf_op jit(solution)/shard_map/triangle/pallas_call | solution.py:584
  126.6 1.2 copy.7
